TPU v7x, 256 devices: a whole 4x4x8 slice. The times are simulated.
256 devices in a mesh: blk: 8 (over x_hi, y), tok: 32 (over x_lo, z, core).
Axes of the slice: x: 4 (x_hi: 2, x_lo: 2; x = x_hi * 2 + x_lo), y: 4, z: 8, core: 2. Of those that a mesh axis runs over, the one named last changes fastest.
Arguments:
- states: bfloat16 [1024, 3584], P('tok'), may hold values from -30 to 30
- head: bfloat16 [3584, 262144], P(None, ('blk', 'tok')), may hold values from -0.2 to 0.2
- targets: int32 [1024], P('tok'), may hold values from 0 to 262143
- ref_loss: float32 [1024], P('tok'), may hold values from 0 to 8
- seq_ids: int32 [1024], P('tok'), may hold values from 0 to 511, never falling along the last dimension, each value on 1 to 4 neighbouring positions
Outputs:
- excess: float32 [1024], P('tok')
- seq_score: float32 [512], replicated
Inputs may be any that keep to these rules, and one draw needn't show every extreme that they name: `seq_ids`: sequence numbers never fall along the tokens; every number from 0 to 511 occurs, on 1 to 4 consecutive tokens.
All inputs are finite; a program needn't handle non-finite values.
Results may differ from a plain program's by a relative error of at most 0.0003.
Values may be sent and summed in bfloat16 or wider, within the bound.
No kernel may reach another device: no remote copies, remote signals or barrier semaphores. Data moves between devices by JAX's collectives and lax.ppermute only.
A program may use at most 64 MiB of HBM per device.

v0:
```python
import functools

import jax
import jax.numpy as jnp
from jax import lax
from jax.experimental import pallas as pl
from jax.experimental.pallas import tpu as pltpu
from jax.sharding import Mesh
from jax.sharding import PartitionSpec as P


TOK = ("xl", "z", "c")
BLK_TOK = ("xh", "y", "xl", "z", "c")
X = ("xh", "xl")
PLANE = ("xh", "xl", "y")
LANES = 128
TILE = 256
VMEM_BYTES = 67043328

VMEM = pl.BlockSpec(memory_space=pltpu.VMEM)
SMEM = pl.BlockSpec(memory_space=pltpu.SMEM)
HBM = pl.BlockSpec(memory_space=pltpu.HBM)


def hop(value, axis, step):
    n = lax.axis_size(axis)
    return lax.ppermute(value, axis, [(i, (i + step) % n) for i in range(n)])


def exchange(copies, axis):
    return lax.all_to_all(copies, axis, 0, 0, tiled=True)


def tag_kernel(states_in, targets_in, loss_in, seq_in, out_ref, targets_ref, loss_ref, seq_ref, sems):
    local, depth = states_in.shape
    pairs = (
        (targets_in, targets_ref),
        (loss_in, loss_ref),
        (seq_in, seq_ref),
        (states_in, out_ref.at[:, pl.ds(0, depth)]),
    )
    copies = [pltpu.make_async_copy(a, b, sems.at[k]) for k, (a, b) in enumerate(pairs)]
    for copy in copies:
        copy.start()
    for copy in copies[:3]:
        copy.wait()
    target, seq, loss = targets_ref[...], seq_ref[...], loss_ref[...]
    high = loss.astype(jnp.bfloat16).astype(jnp.float32)
    middle = (loss - high).astype(jnp.bfloat16).astype(jnp.float32)
    tags = [target >> 16, (target >> 8) & 255, target & 255, seq >> 8, seq & 255]
    tags = [t.astype(jnp.float32) for t in tags] + [high, middle, loss - high - middle]
    row = lax.broadcasted_iota(jnp.int32, (LANES, local), 0)
    columns = jnp.zeros((LANES, local), jnp.float32)
    for k, tag in enumerate(tags):
        columns = jnp.where(row == k, tag, columns)
    columns = jnp.concatenate([columns, jnp.zeros((LANES, LANES - local), jnp.float32)], axis=1)
    out_ref[:, depth:] = columns.T[:local].astype(jnp.bfloat16)
    copies[3].wait()


def score_kernel(index_ref, a_ref, b_ref, *refs):
    *blocks, stats_ref, meta_ref, x_ref, tiles, logits, peak, sems = refs
    rows, depth = x_ref.shape[0], a_ref.shape[0]
    per_head = a_ref.shape[1] // TILE
    count = 2 * per_head
    for j in range(count):
        source = (a_ref, b_ref)[j // per_head].at[:, pl.ds(j % per_head * TILE, TILE)]
        pltpu.make_async_copy(source, tiles.at[j], sems.at[j]).start()
    peak[...] = jnp.full(peak.shape, -jnp.inf, jnp.float32)
    for k, block in enumerate(blocks):
        place = pl.multiple_of(index_ref[3 + k], 16)
        x_ref[pl.ds(place, block.shape[0]), :] = block[...]

    def multiply(j, carry):
        pltpu.make_async_copy(a_ref.at[:, pl.ds(0, TILE)], tiles.at[j], sems.at[j]).wait()
        part = jnp.dot(x_ref[:, :depth], tiles[j], preferred_element_type=jnp.float32)
        logits[j] = part
        top = peak[...]
        for h in range(TILE // LANES):
            top = jnp.maximum(top, part[:, h * LANES : (h + 1) * LANES])
        peak[...] = top
        return carry

    lax.fori_loop(0, count, multiply, 0)

    lane = lax.broadcasted_iota(jnp.int32, (1, LANES), 1).astype(jnp.float32)

    def read(tags, scales):
        weight = jnp.zeros(lane.shape, jnp.float32)
        for k, scale in scales:
            weight = jnp.where(lane == k, scale, weight)
        return tags * weight

    for r in range(rows // LANES):
        span = pl.ds(r * LANES, LANES)
        tags = x_ref[span, depth : depth + LANES].astype(jnp.float32)
        target = jnp.sum(read(tags, ((0, 65536.0), (1, 256.0), (2, 1.0))), axis=1, keepdims=True)
        top = peak[span, :]
        highest = jnp.max(top, axis=1, keepdims=True)
        scaled = jnp.zeros((LANES, LANES), jnp.float32)
        picked = jnp.zeros((LANES, LANES), jnp.float32)
        for j in range(count):
            for h in range(TILE // LANES):
                part = logits[j, span, h * LANES : (h + 1) * LANES]
                scaled += jnp.exp(part - highest)
                first = index_ref[j // per_head] + (j % per_head * TILE + h * LANES)
                picked += jnp.where(lane == target - first.astype(jnp.float32), part, 0.0)
        lse = jnp.max(top.T, axis=0, keepdims=True) + jnp.log(
            jnp.sum(scaled.T, axis=0, keepdims=True)
        )
        chosen = jnp.sum(picked.T, axis=0, keepdims=True)
        for k in range(stats_ref.shape[0]):
            stats_ref[k, :, r * LANES : (r + 1) * LANES] = lse
            stats_ref[k, :, rows + r * LANES : rows + (r + 1) * LANES] = chosen
        seq = jnp.sum(read(tags, ((3, 256.0), (4, 1.0))).T, axis=0, keepdims=True)
        parts = tags.T
        meta_ref[0:1, r * LANES : (r + 1) * LANES] = seq
        meta_ref[1:2, r * LANES : (r + 1) * LANES] = parts[5:6] + parts[6:7] + parts[7:8]


def merged(parts_ref):
    n, _, width = parts_ref.shape
    rows = width // 2
    lses = [parts_ref[k, :, :rows] for k in range(n)]
    highest = functools.reduce(jnp.maximum, lses)
    lse = highest + jnp.log(sum(jnp.exp(l - highest) for l in lses))
    return lse, sum(parts_ref[k, :, rows:] for k in range(n))


def merge_kernel(parts_ref, out_ref):
    lse, picked = merged(parts_ref)
    rows = lse.shape[1]
    for k in range(out_ref.shape[0]):
        out_ref[k, :, :rows] = lse
        out_ref[k, :, rows:] = picked


def finish_kernel(index_ref, parts_ref, meta_ref, own_ref, sums_ref):
    lse, picked = merged(parts_ref)
    excess = lse - picked - meta_ref[1:2, :]
    rows, count = excess.shape[1], sums_ref.shape[1]
    own_ref[...] = pltpu.roll(excess, lax.rem(rows - index_ref[2], rows), 1)[:, :LANES]
    seq = lax.broadcasted_iota(jnp.int32, (count, rows), 0).astype(jnp.float32)
    member = (seq == meta_ref[0:1, :]).astype(jnp.float32)
    left = jnp.concatenate([excess, jnp.ones_like(excess)], axis=0)
    left = jnp.concatenate([left, jnp.zeros((6, rows), jnp.float32)], axis=0)
    sums = lax.dot_general(
        left, member, (((1,), (1,)), ((), ())),
        precision=lax.Precision.HIGHEST, preferred_element_type=jnp.float32,
    )
    sums_ref[...] = sums[0:2]


def ratio_kernel(mine_ref, other_ref, out_ref):
    total = mine_ref[...] + other_ref[...]
    out_ref[...] = total[0:1] / total[1:2]


def on_device(states, head, targets, ref_loss, seq_ids):
    xl, z, c = (lax.axis_index(a) for a in TOK)
    nz = lax.axis_size("z")
    half = nz // 2
    local = states.shape[0]
    depth, width = head.shape
    partner_head = hop(head, "c", 1)
    tagged = pl.pallas_call(
        tag_kernel,
        out_shape=jax.ShapeDtypeStruct((local, depth + LANES), jnp.bfloat16),
        in_specs=[HBM] * 4,
        out_specs=VMEM,
        scratch_shapes=[
            pltpu.VMEM((1, local), jnp.int32),
            pltpu.VMEM((1, local), jnp.float32),
            pltpu.VMEM((1, local), jnp.int32),
            pltpu.SemaphoreType.DMA((4,)),
        ],
        compiler_params=pltpu.CompilerParams(
            vmem_limit_bytes=VMEM_BYTES - 3 * local * (depth + LANES)
        ),
        name="tag",
    )(states, targets[None], ref_loss[None], seq_ids[None])

    up = down = tagged
    mid = local // 2
    blocks, where = [tagged], [(0, 0, 0)]
    for d in range(1, half + 1):
        skip = 0
        if d == half:
            up, down, skip = up[:mid], down[mid:], mid
        up = hop(up, "z", 1)
        down = hop(down, "z", -1)
        if d == 1:
            blocks.append(hop(tagged, X, 1))
            where.append((0, 1, 0))
        far_up = hop(up, X, 1)
        far_down = hop(down, X, -1)
        blocks += [up, down, far_up, far_down]
        where += [(-d, 0, 0), (d, 0, skip), (-d, 1, 0), (d, 1, skip)]

    block = lax.axis_index(("xh", "y")) * lax.axis_size(TOK) + (xl * nz + z) * 2
    distance, other, skip = jnp.asarray([(0, 0, 0)] * 3 + where, jnp.int32).T
    k = lax.iota(jnp.int32, distance.shape[0])
    index = ((xl ^ other) * nz + ((z + distance) & (nz - 1))) * local + skip
    index = jnp.where(k == 0, (block + c) * width, index)
    index = jnp.where(k == 1, (block + 1 - c) * width, index)
    tokens = 2 * nz * local
    plane = lax.axis_size(PLANE)
    count = 2 * width // TILE
    stats, meta = pl.pallas_call(
        score_kernel,
        out_shape=(
            jax.ShapeDtypeStruct((nz, 1, 2 * tokens), jnp.float32),
            jax.ShapeDtypeStruct((2, tokens), jnp.float32),
        ),
        in_specs=[SMEM, HBM, HBM] + [VMEM] * len(blocks),
        out_specs=(VMEM, VMEM),
        scratch_shapes=[
            pltpu.VMEM((tokens, depth + LANES), jnp.bfloat16),
            pltpu.VMEM((count, depth, TILE), jnp.bfloat16),
            pltpu.VMEM((count, tokens, TILE), jnp.float32),
            pltpu.VMEM((tokens, LANES), jnp.float32),
            pltpu.SemaphoreType.DMA((count,)),
        ],
        compiler_params=pltpu.CompilerParams(vmem_limit_bytes=48 << 20),
        cost_estimate=pl.CostEstimate(
            flops=4 * tokens * depth * width, bytes_accessed=4 * depth * width, transcendentals=0
        ),
        name="score",
    )(index, head, partner_head, *blocks)
    stats = pl.pallas_call(
        merge_kernel,
        out_shape=jax.ShapeDtypeStruct((plane, 1, 2 * tokens), jnp.float32),
        in_specs=[VMEM],
        out_specs=VMEM,
        compiler_params=pltpu.CompilerParams(vmem_limit_bytes=2 << 20),
        name="merge",
    )(exchange(stats, "z"))
    own, sums = pl.pallas_call(
        finish_kernel,
        out_shape=(
            jax.ShapeDtypeStruct((1, LANES), jnp.float32),
            jax.ShapeDtypeStruct((2, tokens), jnp.float32),
        ),
        in_specs=[SMEM, VMEM, VMEM],
        out_specs=(VMEM, VMEM),
        compiler_params=pltpu.CompilerParams(vmem_limit_bytes=4 << 20),
        name="finish",
    )(index, exchange(stats, PLANE), meta)
    ratio = pl.pallas_call(
        ratio_kernel,
        out_shape=jax.ShapeDtypeStruct((1, tokens), jnp.float32),
        in_specs=[VMEM, VMEM],
        out_specs=VMEM,
        compiler_params=pltpu.CompilerParams(vmem_limit_bytes=2 << 20),
        name="ratio",
    )(sums, hop(sums, "c", 1))
    return own[0, :local], ratio[0]


def solution(mesh):
    torus = Mesh(mesh.devices.reshape(2, 4, 2, 8, 2), BLK_TOK)
    return jax.shard_map(
        on_device,
        mesh=torus,
        in_specs=(P(TOK, None), P(None, BLK_TOK), P(TOK), P(TOK), P(TOK)),
        out_specs=(P(TOK), P()),
        check_vma=False,
    )
```

profile of v0, /device:TPU:1, one launch (start us, length us, event | category | flops | bytes accessed | tf_op | source)
XLA Modules:
  0.0 93.8 jit_solution(5264795644109667718)
XLA Ops:
  0.6 3.3 %collective-permute-start = (bf16[3584,1024]{1,0:T(8,128)(2,1)}, bf16[3584,1024]{1,0:T(8,128)(2,1)}, u32[]{:S(2)}, u32[]{:S(2)}) collective-permute-start(bf16[3584,1024]{1,0:T(8,128)(2,1)} %a_ref.1), channel_id=1, source_target_pairs={{0,1},{1,0},{2,3},{3,2},{4,5},{5,4},{6,7},{7,6},{8,9},{9,8},{10,11... | collective-permute-start | bytes 22020104 | tf_op jit(solution)/shard_map/ppermute | solution.py:27
  3.9 1.7 %tag.1.refs_0_ = bf16[32,3712]{1,0:T(8,128)(2,1)} custom-call(bf16[32,3584]{1,0:T(8,128)(2,1)} %states_in.1, s32[1,32]{1,0:T(1,128)} %bitcast.9, f32[1,32]{1,0:T(1,128)} %bitcast.10, s32[1,32]{1,0:T(1,128)} %bitcast.11), custom_call_target="tpu_custom_call" | custom-call | tf_op jit(solution)/shard_map/tag/pallas_call | solution.py:166
  5.6 3.9 %collective-permute-start.3 = (bf16[32,3712]{1,0:T(8,128)(2,1)}, bf16[32,3712]{1,0:T(8,128)(2,1)S(1)}, u32[]{:S(2)}, u32[]{:S(2)}) collective-permute-start(bf16[32,3712]{1,0:T(8,128)(2,1)} %tag.1.refs_0_), channel_id=1, source_target_pairs={{0,14},{2,0},{4,2},{6,4},{8,6},{10,8},{12,10},{14,12},{1,15},{3,1}... | collective-permute-start | bytes 712712 | tf_op jit(solution)/shard_map/ppermute | solution.py:27
  9.6 0.0 collective-permute-start.2
  9.6 5.4 %collective-permute-done.3.refs_3_ = bf16[32,3712]{1,0:T(8,128)(2,1)S(1)} collective-permute-done((bf16[32,3712]{1,0:T(8,128)(2,1)}, bf16[32,3712]{1,0:T(8,128)(2,1)S(1)}, u32[]{:S(2)}, u32[]{:S(2)}) %collective-permute-start.3) | collective-permute-done | bytes 237600 | tf_op jit(solution)/shard_map/ppermute | solution.py:27
  15.0 3.3 %collective-permute-start.7 = (bf16[32,3712]{1,0:T(8,128)(2,1)S(1)}, bf16[32,3712]{1,0:T(8,128)(2,1)S(1)}, u32[]{:S(2)}, u32[]{:S(2)}) collective-permute-start(bf16[32,3712]{1,0:T(8,128)(2,1)S(1)} %collective-permute-done.3.refs_3_), channel_id=1, source_target_pairs={{0,14},{2,0},{4,2},{6,4},{8,6},{10,8},{12,10},{14,12},{1,15},{3,1}... | collective-permute-start | bytes 712712 | tf_op jit(solution)/shard_map/ppermute | solution.py:27
  18.3 0.0 collective-permute-done.2.refs_2_
  18.3 1.2 %collective-permute-start.1 = (bf16[32,3712]{1,0:T(8,128)(2,1)}, bf16[32,3712]{1,0:T(8,128)(2,1)S(1)}, u32[]{:S(2)}, u32[]{:S(2)}) collective-permute-start(bf16[32,3712]{1,0:T(8,128)(2,1)} %tag.1.refs_0_), channel_id=1, source_target_pairs={{0,16},{16,128},{128,144},{144,0},{1,17},{17,129},{129,145},{145,1... | collective-permute-start | bytes 712712 | tf_op jit(solution)/shard_map/ppermute | solution.py:27
  19.5 3.0 %collective-permute-done.7.refs_7_ = bf16[32,3712]{1,0:T(8,128)(2,1)S(1)} collective-permute-done((bf16[32,3712]{1,0:T(8,128)(2,1)S(1)}, bf16[32,3712]{1,0:T(8,128)(2,1)S(1)}, u32[]{:S(2)}, u32[]{:S(2)}) %collective-permute-start.7) | collective-permute-done | bytes 237600 | tf_op jit(solution)/shard_map/ppermute | solution.py:27
  22.6 3.4 %collective-permute-start.11 = (bf16[32,3712]{1,0:T(8,128)(2,1)S(1)}, bf16[32,3712]{1,0:T(8,128)(2,1)S(1)}, u32[]{:S(2)}, u32[]{:S(2)}) collective-permute-start(bf16[32,3712]{1,0:T(8,128)(2,1)S(1)} %collective-permute-done.7.refs_7_), channel_id=1, source_target_pairs={{0,14},{2,0},{4,2},{6,4},{8,6},{10,8},{12,10},{14,12},{1,15},{3,1}... | collective-permute-start | bytes 712712 | tf_op jit(solution)/shard_map/ppermute | solution.py:27
  26.0 2.5 %collective-permute-start.5 = (bf16[32,3712]{1,0:T(8,128)(2,1)S(1)}, bf16[32,3712]{1,0:T(8,128)(2,1)S(1)}, u32[]{:S(2)}, u32[]{:S(2)}) collective-permute-start(bf16[32,3712]{1,0:T(8,128)(2,1)S(1)} %collective-permute-done.3.refs_3_), channel_id=1, source_target_pairs={{0,144},{16,0},{128,16},{144,128},{1,145},{17,1},{129,17},{145,129... | collective-permute-start | bytes 712712 | tf_op jit(solution)/shard_map/ppermute | solution.py:27
  28.5 0.9 collective-permute-done.11.refs_11_
  29.4 2.5 %collective-permute-start.9 = (bf16[32,3712]{1,0:T(8,128)(2,1)S(1)}, bf16[32,3712]{1,0:T(8,128)(2,1)S(1)}, u32[]{:S(2)}, u32[]{:S(2)}) collective-permute-start(bf16[32,3712]{1,0:T(8,128)(2,1)S(1)} %collective-permute-done.7.refs_7_), channel_id=1, source_target_pairs={{0,144},{16,0},{128,16},{144,128},{1,145},{17,1},{129,17},{145,129... | collective-permute-start | bytes 712712 | tf_op jit(solution)/shard_map/ppermute | solution.py:27
  31.9 0.7 collective-permute-done.10.refs_10_
  32.5 1.2 %collective-permute-start.8 = (bf16[32,3712]{1,0:T(8,128)(2,1)S(1)}, bf16[32,3712]{1,0:T(8,128)(2,1)S(1)}, u32[]{:S(2)}, u32[]{:S(2)}) collective-permute-start(bf16[32,3712]{1,0:T(8,128)(2,1)S(1)} %collective-permute-done.6.refs_6_), channel_id=1, source_target_pairs={{0,16},{16,128},{128,144},{144,0},{1,17},{17,129},{129,145},{145,1... | collective-permute-start | bytes 712712 | tf_op jit(solution)/shard_map/ppermute | solution.py:27
  33.7 0.7 slice.13
  34.4 1.6 %collective-permute-start.15 = (bf16[16,3712]{1,0:T(8,128)(2,1)}, bf16[16,3712]{1,0:T(8,128)(2,1)S(1)}, u32[]{:S(2)}, u32[]{:S(2)}) collective-permute-start(bf16[16,3712]{1,0:T(8,128)(2,1)} %slice.13), channel_id=1, source_target_pairs={{0,14},{2,0},{4,2},{6,4},{8,6},{10,8},{12,10},{14,12},{1,15},{3,1}... | collective-permute-start | bytes 356360 | tf_op jit(solution)/shard_map/ppermute | solution.py:27
  36.1 1.4 %collective-permute-done.9.refs_9_ = bf16[32,3712]{1,0:T(8,128)(2,1)S(1)} collective-permute-done((bf16[32,3712]{1,0:T(8,128)(2,1)S(1)}, bf16[32,3712]{1,0:T(8,128)(2,1)S(1)}, u32[]{:S(2)}, u32[]{:S(2)}) %collective-permute-start.9) | collective-permute-done | bytes 237600 | tf_op jit(solution)/shard_map/ppermute | solution.py:27
  37.5 3.4 %collective-permute-start.13 = (bf16[32,3712]{1,0:T(8,128)(2,1)S(1)}, bf16[32,3712]{1,0:T(8,128)(2,1)S(1)}, u32[]{:S(2)}, u32[]{:S(2)}) collective-permute-start(bf16[32,3712]{1,0:T(8,128)(2,1)S(1)} %collective-permute-done.11.refs_11_), channel_id=1, source_target_pairs={{0,144},{16,0},{128,16},{144,128},{1,145},{17,1},{129,17},{145,129... | collective-permute-start | bytes 712712 | tf_op jit(solution)/shard_map/ppermute | solution.py:27
  40.9 2.7 %collective-permute-start.17 = (bf16[16,3712]{1,0:T(8,128)(2,1)S(1)}, bf16[16,3712]{1,0:T(8,128)(2,1)S(1)}, u32[]{:S(2)}, u32[]{:S(2)}) collective-permute-start(bf16[16,3712]{1,0:T(8,128)(2,1)S(1)} %collective-permute-done.15.refs_15_), channel_id=1, source_target_pairs={{0,144},{16,0},{128,16},{144,128},{1,145},{17,1},{129,17},{145,129... | collective-permute-start | bytes 356360 | tf_op jit(solution)/shard_map/ppermute | solution.py:27
  43.6 0.7 compare_select_fusion.1.index_ref
  44.3 2.3 %collective-permute-done.17.refs_17_ = bf16[16,3712]{1,0:T(8,128)(2,1)S(1)} collective-permute-done((bf16[16,3712]{1,0:T(8,128)(2,1)S(1)}, bf16[16,3712]{1,0:T(8,128)(2,1)S(1)}, u32[]{:S(2)}, u32[]{:S(2)}) %collective-permute-start.17) | collective-permute-done | bytes 118816 | tf_op jit(solution)/shard_map/ppermute | solution.py:27
  46.6 3.3 %collective-permute-done.16.refs_16_ = bf16[16,3712]{1,0:T(8,128)(2,1)S(1)} collective-permute-done((bf16[16,3712]{1,0:T(8,128)(2,1)S(1)}, bf16[16,3712]{1,0:T(8,128)(2,1)S(1)}, u32[]{:S(2)}, u32[]{:S(2)}) %collective-permute-start.16) | collective-permute-done | bytes 118816 | tf_op jit(solution)/shard_map/ppermute | solution.py:27
  49.9 0.9 %copy-done = bf16[32,3712]{1,0:T(8,128)(2,1)S(1)} copy-done((bf16[32,3712]{1,0:T(8,128)(2,1)S(1)}, bf16[32,3712]{1,0:T(8,128)(2,1)}, u32[]{:S(2)}) %copy-start) | copy-done | bytes 237592
  50.8 12.5 %score.1 = (f32[8,1,1024]{2,1,0:T(1,128)S(1)}, f32[2,512]{1,0:T(2,128)S(1)}) custom-call(s32[21]{0:T(128)S(1)} %compare_select_fusion.1.index_ref, bf16[3584,1024]{1,0:T(8,128)(2,1)} %a_ref.1, bf16[3584,1024]{1,0:T(8,128)(2,1)} %collective-permute-done.b_ref, bf16[32,3712]{1,0:T(8,128)(2,1)S(1)} %copy-done, ...), custom_call_target="tpu_custom_call" | custom-call | flops 7516192768 | bytes 14680064 | tf_op jit(solution)/shard_map/score/pallas_call | solution.py:209
  63.3 11.0 %all_to_all.10.parts_ref = f32[8,1,1024]{2,1,0:T(1,128)S(1)} all-to-all(f32[8,1,1024]{2,1,0:T(1,128)S(1)} %get-tuple-element.6), channel_id=1, replica_groups=mesh['xh'=2,'y'=4,'xl'=2,'z'=8,'c'=2] {'z'}, dimensions={0} | all-to-all | bytes 65536 | tf_op jit(solution)/shard_map/all_to_all | solution.py:31
  74.4 10.6 %all_to_all.11.parts_ref = f32[16,1,1024]{2,1,0:T(1,128)S(1)} all-to-all(f32[16,1,1024]{2,1,0:T(1,128)S(1)} %merge.1), channel_id=1, replica_groups=mesh['xh'=2,'y'=4,'xl'=2,'z'=8,'c'=2] {'xh','xl','y'}, dimensions={0} | all-to-all | bytes 131072 | tf_op jit(solution)/shard_map/all_to_all | solution.py:31
  85.0 1.5 %finish.1 = (f32[1,128]{1,0:T(1,128)S(1)}, f32[2,512]{1,0:T(2,128)S(1)}) custom-call(s32[21]{0:T(128)S(1)} %compare_select_fusion.1.index_ref, f32[16,1,1024]{2,1,0:T(1,128)S(1)} %all_to_all.11.parts_ref, f32[2,512]{1,0:T(2,128)S(1)} %get-tuple-element.7.meta_ref), custom_call_target="tpu_custom_call" | custom-call | tf_op jit(solution)/shard_map/finish/pallas_call | solution.py:238
  86.5 5.9 %collective-permute-start.18 = (f32[2,512]{1,0:T(2,128)S(1)}, f32[2,512]{1,0:T(2,128)S(1)}, u32[]{:S(2)}, u32[]{:S(2)}) collective-permute-start(f32[2,512]{1,0:T(2,128)S(1)} %get-tuple-element.9.mine_ref), channel_id=1, source_target_pairs={{0,1},{1,0},{2,3},{3,2},{4,5},{5,4},{6,7},{7,6},{8,9},{9,8},{10,11... | collective-permute-start | bytes 12296 | tf_op jit(solution)/shard_map/ppermute | solution.py:27
  92.4 0.5 slice_bitcast_fusion
  92.9 0.3 collective-permute-done.18.other_ref
  93.2 0.6 ratio.1
  (19 shorter events, 0.1 us)
Async XLA Ops:
  0.6 49.3 %collective-permute-start = (bf16[3584,1024]{1,0:T(8,128)(2,1)}, bf16[3584,1024]{1,0:T(8,128)(2,1)}, u32[]{:S(2)}, u32[]{:S(2)}) collective-permute-start(bf16[3584,1024]{1,0:T(8,128)(2,1)} %a_ref.1), channel_id=1, source_target_pairs={{0,1},{1,0},{2,3},{3,2},{4,5},{5,4},{6,7},{7,6},{8,9},{9,8},{10,11... | collective-permute-start | bytes 22020104 | tf_op jit(solution)/shard_map/ppermute | solution.py:27
  5.6 9.4 %collective-permute-start.3 = (bf16[32,3712]{1,0:T(8,128)(2,1)}, bf16[32,3712]{1,0:T(8,128)(2,1)S(1)}, u32[]{:S(2)}, u32[]{:S(2)}) collective-permute-start(bf16[32,3712]{1,0:T(8,128)(2,1)} %tag.1.refs_0_), channel_id=1, source_target_pairs={{0,14},{2,0},{4,2},{6,4},{8,6},{10,8},{12,10},{14,12},{1,15},{3,1}... | collective-permute-start | bytes 712712 | tf_op jit(solution)/shard_map/ppermute | solution.py:27
  9.6 8.7 %collective-permute-start.2 = (bf16[32,3712]{1,0:T(8,128)(2,1)}, bf16[32,3712]{1,0:T(8,128)(2,1)S(1)}, u32[]{:S(2)}, u32[]{:S(2)}) collective-permute-start(bf16[32,3712]{1,0:T(8,128)(2,1)} %tag.1.refs_0_), channel_id=1, source_target_pairs={{0,2},{2,4},{4,6},{6,8},{8,10},{10,12},{12,14},{14,0},{1,3},{3,5},... | collective-permute-start | bytes 712712 | tf_op jit(solution)/shard_map/ppermute | solution.py:27
  15.0 7.6 %collective-permute-start.7 = (bf16[32,3712]{1,0:T(8,128)(2,1)S(1)}, bf16[32,3712]{1,0:T(8,128)(2,1)S(1)}, u32[]{:S(2)}, u32[]{:S(2)}) collective-permute-start(bf16[32,3712]{1,0:T(8,128)(2,1)S(1)} %collective-permute-done.3.refs_3_), channel_id=1, source_target_pairs={{0,14},{2,0},{4,2},{6,4},{8,6},{10,8},{12,10},{14,12},{1,15},{3,1}... | collective-permute-start | bytes 712712 | tf_op jit(solution)/shard_map/ppermute | solution.py:27
  18.3 7.7 %collective-permute-start.6 = (bf16[32,3712]{1,0:T(8,128)(2,1)S(1)}, bf16[32,3712]{1,0:T(8,128)(2,1)S(1)}, u32[]{:S(2)}, u32[]{:S(2)}) collective-permute-start(bf16[32,3712]{1,0:T(8,128)(2,1)S(1)} %collective-permute-done.2.refs_2_), channel_id=1, source_target_pairs={{0,2},{2,4},{4,6},{6,8},{8,10},{10,12},{12,14},{14,0},{1,3},{3,5},... | collective-permute-start | bytes 712712 | tf_op jit(solution)/shard_map/ppermute | solution.py:27
  18.3 10.2 %collective-permute-start.1 = (bf16[32,3712]{1,0:T(8,128)(2,1)}, bf16[32,3712]{1,0:T(8,128)(2,1)S(1)}, u32[]{:S(2)}, u32[]{:S(2)}) collective-permute-start(bf16[32,3712]{1,0:T(8,128)(2,1)} %tag.1.refs_0_), channel_id=1, source_target_pairs={{0,16},{16,128},{128,144},{144,0},{1,17},{17,129},{129,145},{145,1... | collective-permute-start | bytes 712712 | tf_op jit(solution)/shard_map/ppermute | solution.py:27
  22.6 6.8 %collective-permute-start.11 = (bf16[32,3712]{1,0:T(8,128)(2,1)S(1)}, bf16[32,3712]{1,0:T(8,128)(2,1)S(1)}, u32[]{:S(2)}, u32[]{:S(2)}) collective-permute-start(bf16[32,3712]{1,0:T(8,128)(2,1)S(1)} %collective-permute-done.7.refs_7_), channel_id=1, source_target_pairs={{0,14},{2,0},{4,2},{6,4},{8,6},{10,8},{12,10},{14,12},{1,15},{3,1}... | collective-permute-start | bytes 712712 | tf_op jit(solution)/shard_map/ppermute | solution.py:27
  26.0 6.5 %collective-permute-start.10 = (bf16[32,3712]{1,0:T(8,128)(2,1)S(1)}, bf16[32,3712]{1,0:T(8,128)(2,1)S(1)}, u32[]{:S(2)}, u32[]{:S(2)}) collective-permute-start(bf16[32,3712]{1,0:T(8,128)(2,1)S(1)} %collective-permute-done.6.refs_6_), channel_id=1, source_target_pairs={{0,2},{2,4},{4,6},{6,8},{8,10},{10,12},{12,14},{14,0},{1,3},{3,5},... | collective-permute-start | bytes 712712 | tf_op jit(solution)/shard_map/ppermute | solution.py:27
  26.0 8.4 %collective-permute-start.5 = (bf16[32,3712]{1,0:T(8,128)(2,1)S(1)}, bf16[32,3712]{1,0:T(8,128)(2,1)S(1)}, u32[]{:S(2)}, u32[]{:S(2)}) collective-permute-start(bf16[32,3712]{1,0:T(8,128)(2,1)S(1)} %collective-permute-done.3.refs_3_), channel_id=1, source_target_pairs={{0,144},{16,0},{128,16},{144,128},{1,145},{17,1},{129,17},{145,129... | collective-permute-start | bytes 712712 | tf_op jit(solution)/shard_map/ppermute | solution.py:27
  28.5 7.6 %collective-permute-start.4 = (bf16[32,3712]{1,0:T(8,128)(2,1)S(1)}, bf16[32,3712]{1,0:T(8,128)(2,1)S(1)}, u32[]{:S(2)}, u32[]{:S(2)}) collective-permute-start(bf16[32,3712]{1,0:T(8,128)(2,1)S(1)} %collective-permute-done.2.refs_2_), channel_id=1, source_target_pairs={{0,16},{16,128},{128,144},{144,0},{1,17},{17,129},{129,145},{145,1... | collective-permute-start | bytes 712712 | tf_op jit(solution)/shard_map/ppermute | solution.py:27
  29.4 8.1 %collective-permute-start.9 = (bf16[32,3712]{1,0:T(8,128)(2,1)S(1)}, bf16[32,3712]{1,0:T(8,128)(2,1)S(1)}, u32[]{:S(2)}, u32[]{:S(2)}) collective-permute-start(bf16[32,3712]{1,0:T(8,128)(2,1)S(1)} %collective-permute-done.7.refs_7_), channel_id=1, source_target_pairs={{0,144},{16,0},{128,16},{144,128},{1,145},{17,1},{129,17},{145,129... | collective-permute-start | bytes 712712 | tf_op jit(solution)/shard_map/ppermute | solution.py:27
  32.5 8.4 %collective-permute-start.8 = (bf16[32,3712]{1,0:T(8,128)(2,1)S(1)}, bf16[32,3712]{1,0:T(8,128)(2,1)S(1)}, u32[]{:S(2)}, u32[]{:S(2)}) collective-permute-start(bf16[32,3712]{1,0:T(8,128)(2,1)S(1)} %collective-permute-done.6.refs_6_), channel_id=1, source_target_pairs={{0,16},{16,128},{128,144},{144,0},{1,17},{17,129},{129,145},{145,1... | collective-permute-start | bytes 712712 | tf_op jit(solution)/shard_map/ppermute | solution.py:27
  34.4 6.5 %collective-permute-start.15 = (bf16[16,3712]{1,0:T(8,128)(2,1)}, bf16[16,3712]{1,0:T(8,128)(2,1)S(1)}, u32[]{:S(2)}, u32[]{:S(2)}) collective-permute-start(bf16[16,3712]{1,0:T(8,128)(2,1)} %slice.13), channel_id=1, source_target_pairs={{0,14},{2,0},{4,2},{6,4},{8,6},{10,8},{12,10},{14,12},{1,15},{3,1}... | collective-permute-start | bytes 356360 | tf_op jit(solution)/shard_map/ppermute | solution.py:27
  36.1 7.5 %collective-permute-start.14 = (bf16[16,3712]{1,0:T(8,128)(2,1)S(1)}, bf16[16,3712]{1,0:T(8,128)(2,1)S(1)}, u32[]{:S(2)}, u32[]{:S(2)}) collective-permute-start(bf16[16,3712]{1,0:T(8,128)(2,1)S(1)} %slice.12), channel_id=1, source_target_pairs={{0,2},{2,4},{4,6},{6,8},{8,10},{10,12},{12,14},{14,0},{1,3},{3,5},... | collective-permute-start | bytes 356360 | tf_op jit(solution)/shard_map/ppermute | solution.py:27
  37.5 9.1 %collective-permute-start.13 = (bf16[32,3712]{1,0:T(8,128)(2,1)S(1)}, bf16[32,3712]{1,0:T(8,128)(2,1)S(1)}, u32[]{:S(2)}, u32[]{:S(2)}) collective-permute-start(bf16[32,3712]{1,0:T(8,128)(2,1)S(1)} %collective-permute-done.11.refs_11_), channel_id=1, source_target_pairs={{0,144},{16,0},{128,16},{144,128},{1,145},{17,1},{129,17},{145,129... | collective-permute-start | bytes 712712 | tf_op jit(solution)/shard_map/ppermute | solution.py:27
  40.9 9.0 %collective-permute-start.12 = (bf16[32,3712]{1,0:T(8,128)(2,1)S(1)}, bf16[32,3712]{1,0:T(8,128)(2,1)S(1)}, u32[]{:S(2)}, u32[]{:S(2)}) collective-permute-start(bf16[32,3712]{1,0:T(8,128)(2,1)S(1)} %collective-permute-done.10.refs_10_), channel_id=1, source_target_pairs={{0,16},{16,128},{128,144},{144,0},{1,17},{17,129},{129,145},{145,1... | collective-permute-start | bytes 712712 | tf_op jit(solution)/shard_map/ppermute | solution.py:27
  40.9 5.7 %collective-permute-start.17 = (bf16[16,3712]{1,0:T(8,128)(2,1)S(1)}, bf16[16,3712]{1,0:T(8,128)(2,1)S(1)}, u32[]{:S(2)}, u32[]{:S(2)}) collective-permute-start(bf16[16,3712]{1,0:T(8,128)(2,1)S(1)} %collective-permute-done.15.refs_15_), channel_id=1, source_target_pairs={{0,144},{16,0},{128,16},{144,128},{1,145},{17,1},{129,17},{145,129... | collective-permute-start | bytes 356360 | tf_op jit(solution)/shard_map/ppermute | solution.py:27
  43.6 6.3 %collective-permute-start.16 = (bf16[16,3712]{1,0:T(8,128)(2,1)S(1)}, bf16[16,3712]{1,0:T(8,128)(2,1)S(1)}, u32[]{:S(2)}, u32[]{:S(2)}) collective-permute-start(bf16[16,3712]{1,0:T(8,128)(2,1)S(1)} %collective-permute-done.14.refs_14_), channel_id=1, source_target_pairs={{0,16},{16,128},{128,144},{144,0},{1,17},{17,129},{129,145},{145,1... | collective-permute-start | bytes 356360 | tf_op jit(solution)/shard_map/ppermute | solution.py:27
  49.9 0.9 %copy-start = (bf16[32,3712]{1,0:T(8,128)(2,1)S(1)}, bf16[32,3712]{1,0:T(8,128)(2,1)}, u32[]{:S(2)}) copy-start(bf16[32,3712]{1,0:T(8,128)(2,1)} %tag.1.refs_0_) | copy-start | bytes 712708
  86.5 6.7 %collective-permute-start.18 = (f32[2,512]{1,0:T(2,128)S(1)}, f32[2,512]{1,0:T(2,128)S(1)}, u32[]{:S(2)}, u32[]{:S(2)}) collective-permute-start(f32[2,512]{1,0:T(2,128)S(1)} %get-tuple-element.9.mine_ref), channel_id=1, source_target_pairs={{0,1},{1,0},{2,3},{3,2},{4,5},{5,4},{6,7},{7,6},{8,9},{9,8},{10,11... | collective-permute-start | bytes 12296 | tf_op jit(solution)/shard_map/ppermute | solution.py:27
where the time goes:
time: 94 us; the launch traced here: 93.8 us
  starting transfers between devices  34.9 us (37%)
  blocking collectives  21.6 us (23%)
  waiting for transfers between devices  17.4 us (19%)
  Pallas kernels  16.3 us (17%)
  local copies, waits for them, and re-layouts  2.12 us (2%)
    ppermute x19, starting transfers between devices, hop(): return lax.ppermute(value, axis, [(i, (i + step) % n) for i in range(n)])  34.9 us
    all_to_all x2, blocking collectives, exchange(): return lax.all_to_all(copies, axis, 0, 0, tiled=True)  21.6 us
    ppermute x19, waiting for transfers between devices, hop(): return lax.ppermute(value, axis, [(i, (i + step) % n) for i in range(n)])  17.4 us
    pallas_call x1, Pallas kernels, on_device(): pl.pallas_call(score_kernel, out_shape=(jax.ShapeDtypeStruct((nz, 1, 2 *...  12.5 us
  transfers between devices with their start and end apart: 19, of which 8 were waited for; matrix products, arithmetic and copies ran while one was open for 2% of the time, Pallas kernels for 2%

commit v1 on v0

--- a/solution.py
+++ b/solution.py
@@ -16,6 +16,7 @@
 LANES = 128
 TILE = 256
 VMEM_BYTES = 67043328
+HEADER = 5
 
 VMEM = pl.BlockSpec(memory_space=pltpu.VMEM)
 SMEM = pl.BlockSpec(memory_space=pltpu.SMEM)
@@ -67,9 +68,16 @@
         source = (a_ref, b_ref)[j // per_head].at[:, pl.ds(j % per_head * TILE, TILE)]
         pltpu.make_async_copy(source, tiles.at[j], sems.at[j]).start()
     peak[...] = jnp.full(peak.shape, -jnp.inf, jnp.float32)
-    for k, block in enumerate(blocks):
-        place = pl.multiple_of(index_ref[3 + k], 16)
-        x_ref[pl.ds(place, block.shape[0]), :] = block[...]
+
+    def take(some):
+        for k in some:
+            place = pl.multiple_of(index_ref[HEADER + k], blocks[k].shape[0])
+            x_ref[pl.ds(place, blocks[k].shape[0]), :] = blocks[k][...]
+
+    first, last = range(4), range(len(blocks) - 4, len(blocks))
+    take(range(4, len(blocks) - 4))
+    pl.when(index_ref[2] == 0)(lambda: take(first))
+    pl.when(index_ref[2] != 0)(lambda: take(last))
 
     def multiply(j, carry):
         pltpu.make_async_copy(a_ref.at[:, pl.ds(0, TILE)], tiles.at[j], sems.at[j]).wait()
@@ -103,8 +111,8 @@
             for h in range(TILE // LANES):
                 part = logits[j, span, h * LANES : (h + 1) * LANES]
                 scaled += jnp.exp(part - highest)
-                first = index_ref[j // per_head] + (j % per_head * TILE + h * LANES)
-                picked += jnp.where(lane == target - first.astype(jnp.float32), part, 0.0)
+                column = index_ref[j // per_head] + (j % per_head * TILE + h * LANES)
+                picked += jnp.where(lane == target - column.astype(jnp.float32), part, 0.0)
         lse = jnp.max(top.T, axis=0, keepdims=True) + jnp.log(
             jnp.sum(scaled.T, axis=0, keepdims=True)
         )
@@ -127,33 +135,64 @@
     return lse, sum(parts_ref[k, :, rows:] for k in range(n))
 
 
-def merge_kernel(parts_ref, out_ref):
+def merge_kernel(parts_ref, meta_ref, out_ref):
     lse, picked = merged(parts_ref)
     rows = lse.shape[1]
     for k in range(out_ref.shape[0]):
-        out_ref[k, :, :rows] = lse
-        out_ref[k, :, rows:] = picked
-
-
-def finish_kernel(index_ref, parts_ref, meta_ref, own_ref, sums_ref):
-    lse, picked = merged(parts_ref)
-    excess = lse - picked - meta_ref[1:2, :]
-    rows, count = excess.shape[1], sums_ref.shape[1]
-    own_ref[...] = pltpu.roll(excess, lax.rem(rows - index_ref[2], rows), 1)[:, :LANES]
-    seq = lax.broadcasted_iota(jnp.int32, (count, rows), 0).astype(jnp.float32)
-    member = (seq == meta_ref[0:1, :]).astype(jnp.float32)
-    left = jnp.concatenate([excess, jnp.ones_like(excess)], axis=0)
-    left = jnp.concatenate([left, jnp.zeros((6, rows), jnp.float32)], axis=0)
-    sums = lax.dot_general(
-        left, member, (((1,), (1,)), ((), ())),
-        precision=lax.Precision.HIGHEST, preferred_element_type=jnp.float32,
-    )
-    sums_ref[...] = sums[0:2]
-
-
-def ratio_kernel(mine_ref, other_ref, out_ref):
-    total = mine_ref[...] + other_ref[...]
-    out_ref[...] = total[0:1] / total[1:2]
+        for i, value in enumerate((lse, picked, meta_ref[0:1, :], meta_ref[1:2, :])):
+            out_ref[k, :, i * rows : (i + 1) * rows] = value
+
+
+def held(z, c, nz):
+    half = nz // 2
+    return {(z - s if c == 0 else z + 1 + s) % nz for s in range(half)}
+
+
+def finish_kernel(index_ref, parts_ref, own_ref, score_ref, *, nz, span):
+    rows, count, half = parts_ref.shape[2] // 4, score_ref.shape[1], nz // 2
+    lane = lax.broadcasted_iota(jnp.int32, (1, rows), 1)
+    slot = lax.rem(lax.div(lane, span), half)
+
+    def field(k, i):
+        return parts_ref[k, :, i * rows : (i + 1) * rows]
+
+    excesses, sums = [], None
+    for low in (True, False):
+        lses, picked = [], jnp.zeros((1, rows), jnp.float32)
+        seq, loss = jnp.zeros((1, rows), jnp.float32), jnp.zeros((1, rows), jnp.float32)
+        for k in range(2 * nz):
+            zs = [z for z in held(k // 2, k % 2, nz) if (z < half) == low]
+            if not zs:
+                continue
+            here = functools.reduce(jnp.logical_or, [slot == z % half for z in zs])
+            lses.append(jnp.where(here, field(k, 0), -jnp.inf))
+            picked += jnp.where(here, field(k, 1), 0.0)
+        for z in range(nz):
+            if (z < half) == low:
+                here = slot == z % half
+                seq = jnp.where(here, field(2 * z, 2), seq)
+                loss = jnp.where(here, field(2 * z, 3), loss)
+        highest = functools.reduce(jnp.maximum, lses)
+        lse = highest + jnp.log(sum(jnp.exp(l - highest) for l in lses))
+        excess = lse - picked - loss
+        excesses.append(excess)
+        ids = lax.broadcasted_iota(jnp.int32, (count, rows), 0).astype(jnp.float32)
+        member = jnp.where(ids == seq, 1.0, 0.0).astype(jnp.bfloat16)
+        high = excess.astype(jnp.bfloat16).astype(jnp.float32)
+        middle = (excess - high).astype(jnp.bfloat16).astype(jnp.float32)
+        pieces = [high, middle, excess - high - middle, jnp.ones_like(excess)]
+        row = lax.broadcasted_iota(jnp.int32, (16, rows), 0)
+        left = jnp.zeros((16, rows), jnp.float32)
+        for i, piece in enumerate(pieces):
+            left = jnp.where(row == i, piece, left)
+        part = lax.dot_general(
+            left.astype(jnp.bfloat16), member, (((1,), (1,)), ((), ())),
+            preferred_element_type=jnp.float32,
+        )
+        sums = part if sums is None else sums + part
+    score_ref[...] = (sums[0:1] + sums[1:2] + sums[2:3]) / sums[3:4]
+    mine = jnp.where(index_ref[4] == 0, excesses[0], excesses[1])
+    own_ref[...] = pltpu.roll(mine, lax.rem(rows - index_ref[3], rows), 1)[:, :LANES]
 
 
 def on_device(states, head, targets, ref_loss, seq_ids):
@@ -162,7 +201,6 @@
     half = nz // 2
     local = states.shape[0]
     depth, width = head.shape
-    partner_head = hop(head, "c", 1)
     tagged = pl.pallas_call(
         tag_kernel,
         out_shape=jax.ShapeDtypeStruct((local, depth + LANES), jnp.bfloat16),
@@ -180,36 +218,43 @@
         name="tag",
     )(states, targets[None], ref_loss[None], seq_ids[None])
 
-    up = down = tagged
-    mid = local // 2
-    blocks, where = [tagged], [(0, 0, 0)]
-    for d in range(1, half + 1):
-        skip = 0
-        if d == half:
-            up, down, skip = up[:mid], down[mid:], mid
-        up = hop(up, "z", 1)
-        down = hop(down, "z", -1)
-        if d == 1:
-            blocks.append(hop(tagged, X, 1))
-            where.append((0, 1, 0))
-        far_up = hop(up, X, 1)
-        far_down = hop(down, X, -1)
-        blocks += [up, down, far_up, far_down]
-        where += [(-d, 0, 0), (d, 0, skip), (-d, 1, 0), (d, 1, skip)]
+    other_half = hop(tagged, "c", 1)
+
+    def along(value, axis, first, second):
+        n = lax.axis_size(axis)
+        pairs = [(2 * i, (i + 1) % n * 2) for i in range(n)] if first else []
+        pairs += [(2 * i + 1, (i - 1) % n * 2 + 1) for i in range(n)] if second else []
+        axes = (axis, "c") if isinstance(axis, str) else (*axis, "c")
+        return lax.ppermute(value, axes, pairs)
+
+    near = [tagged, other_half]
+    blocks, where = [], []
+    for s in range(half + 1):
+        if s > 0:
+            for k in range(2):
+                near[k] = along(near[k], "z", s < half, True)
+        for k in range(2):
+            far = along(near[k], X, s < half, s > 0)
+            blocks += [near[k], far]
+            where += [(s, 0, k), (s, 1, k)]
+    partner_head = hop(head, "c", 1)
 
     block = lax.axis_index(("xh", "y")) * lax.axis_size(TOK) + (xl * nz + z) * 2
-    distance, other, skip = jnp.asarray([(0, 0, 0)] * 3 + where, jnp.int32).T
-    k = lax.iota(jnp.int32, distance.shape[0])
-    index = ((xl ^ other) * nz + ((z + distance) & (nz - 1))) * local + skip
-    index = jnp.where(k == 0, (block + c) * width, index)
-    index = jnp.where(k == 1, (block + 1 - c) * width, index)
+    steps, other, piece = jnp.asarray([(0, 0, 0)] * HEADER + where, jnp.int32).T
+    k = lax.iota(jnp.int32, steps.shape[0])
+    span = 2 * local
+    slot = lax.rem(z + jnp.where(c == 0, nz - steps, steps), half)
+    index = ((xl ^ other) * half + slot) * span + (c ^ piece) * local
+    fixed = ((block + c) * width, (block + 1 - c) * width, c, (xl * half + z % half) * span + c * local, z // half)
+    for i, value in enumerate(fixed):
+        index = jnp.where(k == i, value, index)
     tokens = 2 * nz * local
     plane = lax.axis_size(PLANE)
     count = 2 * width // TILE
     stats, meta = pl.pallas_call(
         score_kernel,
         out_shape=(
-            jax.ShapeDtypeStruct((nz, 1, 2 * tokens), jnp.float32),
+            jax.ShapeDtypeStruct((plane, 1, 2 * tokens), jnp.float32),
             jax.ShapeDtypeStruct((2, tokens), jnp.float32),
         ),
         in_specs=[SMEM, HBM, HBM] + [VMEM] * len(blocks),
@@ -221,7 +266,7 @@
             pltpu.VMEM((tokens, LANES), jnp.float32),
             pltpu.SemaphoreType.DMA((count,)),
         ],
-        compiler_params=pltpu.CompilerParams(vmem_limit_bytes=48 << 20),
+        compiler_params=pltpu.CompilerParams(vmem_limit_bytes=45 << 20),
         cost_estimate=pl.CostEstimate(
             flops=4 * tokens * depth * width, bytes_accessed=4 * depth * width, transcendentals=0
         ),
@@ -229,32 +274,24 @@
     )(index, head, partner_head, *blocks)
     stats = pl.pallas_call(
         merge_kernel,
-        out_shape=jax.ShapeDtypeStruct((plane, 1, 2 * tokens), jnp.float32),
-        in_specs=[VMEM],
+        out_shape=jax.ShapeDtypeStruct((2 * nz, 1, 4 * tokens), jnp.float32),
+        in_specs=[VMEM, VMEM],
         out_specs=VMEM,
         compiler_params=pltpu.CompilerParams(vmem_limit_bytes=2 << 20),
         name="merge",
-    )(exchange(stats, "z"))
-    own, sums = pl.pallas_call(
-        finish_kernel,
+    )(exchange(stats, PLANE), meta)
+    own, score = pl.pallas_call(
+        functools.partial(finish_kernel, nz=nz, span=span),
         out_shape=(
             jax.ShapeDtypeStruct((1, LANES), jnp.float32),
-            jax.ShapeDtypeStruct((2, tokens), jnp.float32),
+            jax.ShapeDtypeStruct((1, tokens), jnp.float32),
         ),
-        in_specs=[SMEM, VMEM, VMEM],
+        in_specs=[SMEM, VMEM],
         out_specs=(VMEM, VMEM),
-        compiler_params=pltpu.CompilerParams(vmem_limit_bytes=4 << 20),
+        compiler_params=pltpu.CompilerParams(vmem_limit_bytes=8 << 20),
         name="finish",
-    )(index, exchange(stats, PLANE), meta)
-    ratio = pl.pallas_call(
-        ratio_kernel,
-        out_shape=jax.ShapeDtypeStruct((1, tokens), jnp.float32),
-        in_specs=[VMEM, VMEM],
-        out_specs=VMEM,
-        compiler_params=pltpu.CompilerParams(vmem_limit_bytes=2 << 20),
-        name="ratio",
-    )(sums, hop(sums, "c", 1))
-    return own[0, :local], ratio[0]
+    )(index, exchange(stats, ("z", "c")))
+    return own[0, :local], score[0]
 
 
 def solution(mesh):

time: 94 us -> 97.2 us (1.034)
  waiting for transfers between devices: 17.4 us -> 10.6 us
  starting transfers between devices: 34.9 us -> 40.4 us
  blocking collectives: 21.6 us -> 26.3 us
    ppermute x0 -> x18, starting transfers between devices: none -> 37 us  [along(): return lax.ppermute(value, axes, pairs)]
    ppermute x19 -> x2, starting transfers between devices: 34.9 us -> 3.39 us  [hop(): return lax.ppermute(value, axis, [(i, (i + step) % n) for i in range(n)])]
    ppermute x19 -> x2, waiting for transfers between devices: 17.4 us -> 6.07 us  [hop(): return lax.ppermute(value, axis, [(i, (i + step) % n) for i in range(n)])]
    all_to_all x2, blocking collectives: 21.6 us -> 26.3 us  [exchange(): return lax.all_to_all(copies, axis, 0, 0, tiled=True)]
    ppermute x0 -> x18, waiting for transfers between devices: none -> 4.53 us  [along(): return lax.ppermute(value, axes, pairs)]
    pallas_call x4 -> x3, Pallas kernels: 14.6 us -> 14.8 us  [the longest x1 13.2 us: on_device(): pl.pallas_call(score_kernel, out_shape=(jax.ShapeDtypeStruct((plane, 1, 2...]
  transfers between devices with their start and end apart: 19 -> 20, of which waited for: 8 -> 3; matrix products, arithmetic and copies ran while one was open for 2% -> 1% of each run, Pallas kernels for 2% -> 2%
where the time goes in v1:
time: 97.2 us; the launch traced here: 96.8 us
  starting transfers between devices  40.4 us (42%)
  blocking collectives  26.3 us (27%)
  Pallas kernels  16.6 us (17%)
  waiting for transfers between devices  10.6 us (11%)
  local copies, waits for them, and re-layouts  1.45 us (1%)
    ppermute x18, starting transfers between devices, along(): return lax.ppermute(value, axes, pairs)  37 us
    all_to_all x2, blocking collectives, exchange(): return lax.all_to_all(copies, axis, 0, 0, tiled=True)  26.3 us
    pallas_call x1, Pallas kernels, on_device(): pl.pallas_call(score_kernel, out_shape=(jax.ShapeDtypeStruct((plane, 1, 2...  13.2 us
    ppermute x2, waiting for transfers between devices, hop(): return lax.ppermute(value, axis, [(i, (i + step) % n) for i in range(n)])  6.07 us
    ppermute x18, waiting for transfers between devices, along(): return lax.ppermute(value, axes, pairs)  4.53 us
    ppermute x2, starting transfers between devices, hop(): return lax.ppermute(value, axis, [(i, (i + step) % n) for i in range(n)])  3.39 us
  transfers between devices with their start and end apart: 20, of which 3 were waited for; matrix products, arithmetic and copies ran while one was open for 1% of the time, Pallas kernels for 2%

profile of v1, /device:TPU:1, one launch (start us, length us, event | category | flops | bytes accessed | tf_op | source)
XLA Modules:
  0.0 96.8 jit_solution(7896106046586444193)
XLA Ops:
  0.6 3.3 %collective-permute-start = (bf16[3584,1024]{1,0:T(8,128)(2,1)}, bf16[3584,1024]{1,0:T(8,128)(2,1)}, u32[]{:S(2)}, u32[]{:S(2)}) collective-permute-start(bf16[3584,1024]{1,0:T(8,128)(2,1)} %a_ref.1), channel_id=1, source_target_pairs={{0,1},{1,0},{2,3},{3,2},{4,5},{5,4},{6,7},{7,6},{8,9},{9,8},{10,11... | collective-permute-start | bytes 22020104 | tf_op jit(solution)/shard_map/ppermute | solution.py:28
  3.9 1.7 %tag.1.refs_0_ = bf16[32,3712]{1,0:T(8,128)(2,1)} custom-call(bf16[32,3584]{1,0:T(8,128)(2,1)} %states_in.1, s32[1,32]{1,0:T(1,128)} %bitcast.14, f32[1,32]{1,0:T(1,128)} %bitcast.15, s32[1,32]{1,0:T(1,128)} %bitcast.16), custom_call_target="tpu_custom_call" | custom-call | tf_op jit(solution)/shard_map/tag/pallas_call | solution.py:204
  5.6 0.1 collective-permute-start.2
  5.8 3.9 %collective-permute-start.4 = (bf16[32,3712]{1,0:T(8,128)(2,1)}, bf16[32,3712]{1,0:T(8,128)(2,1)S(1)}, u32[]{:S(2)}, u32[]{:S(2)}) collective-permute-start(bf16[32,3712]{1,0:T(8,128)(2,1)} %tag.1.refs_0_), channel_id=1, source_target_pairs={{0,2},{2,4},{4,6},{6,8},{8,10},{10,12},{12,14},{14,0},{1,15},{3,1}... | collective-permute-start | bytes 712712 | tf_op jit(solution)/shard_map/ppermute | solution.py:228
  9.7 6.1 %collective-permute-done.2.refs_2_ = bf16[32,3712]{1,0:T(8,128)(2,1)S(1)} collective-permute-done((bf16[32,3712]{1,0:T(8,128)(2,1)}, bf16[32,3712]{1,0:T(8,128)(2,1)S(1)}, u32[]{:S(2)}, u32[]{:S(2)}) %collective-permute-start.2) | collective-permute-done | bytes 237600 | tf_op jit(solution)/shard_map/ppermute | solution.py:28
  15.8 3.9 %collective-permute-start.6 = (bf16[32,3712]{1,0:T(8,128)(2,1)S(1)}, bf16[32,3712]{1,0:T(8,128)(2,1)S(1)}, u32[]{:S(2)}, u32[]{:S(2)}) collective-permute-start(bf16[32,3712]{1,0:T(8,128)(2,1)S(1)} %collective-permute-done.2.refs_2_), channel_id=1, source_target_pairs={{0,2},{2,4},{4,6},{6,8},{8,10},{10,12},{12,14},{14,0},{1,15},{3,1}... | collective-permute-start | bytes 712712 | tf_op jit(solution)/shard_map/ppermute | solution.py:228
  19.6 0.7 collective-permute-start.1
  20.3 0.8 collective-permute-start.8
  21.1 2.5 %collective-permute-start.5 = (bf16[32,3712]{1,0:T(8,128)(2,1)S(1)}, bf16[32,3712]{1,0:T(8,128)(2,1)S(1)}, u32[]{:S(2)}, u32[]{:S(2)}) collective-permute-start(bf16[32,3712]{1,0:T(8,128)(2,1)S(1)} %collective-permute-done.4.refs_4_), channel_id=1, source_target_pairs={{0,16},{16,128},{128,144},{144,0},{1,145},{17,1},{129,17},{145,129... | collective-permute-start | bytes 712712 | tf_op jit(solution)/shard_map/ppermute | solution.py:228
  23.6 0.0 collective-permute-done.6.refs_6_
  23.6 2.2 %collective-permute-start.10 = (bf16[32,3712]{1,0:T(8,128)(2,1)S(1)}, bf16[32,3712]{1,0:T(8,128)(2,1)S(1)}, u32[]{:S(2)}, u32[]{:S(2)}) collective-permute-start(bf16[32,3712]{1,0:T(8,128)(2,1)S(1)} %collective-permute-done.6.refs_6_), channel_id=1, source_target_pairs={{0,2},{2,4},{4,6},{6,8},{8,10},{10,12},{12,14},{14,0},{1,15},{3,1}... | collective-permute-start | bytes 712712 | tf_op jit(solution)/shard_map/ppermute | solution.py:228
  25.8 0.7 collective-permute-start.3
  26.5 2.2 %collective-permute-start.12 = (bf16[32,3712]{1,0:T(8,128)(2,1)S(1)}, bf16[32,3712]{1,0:T(8,128)(2,1)S(1)}, u32[]{:S(2)}, u32[]{:S(2)}) collective-permute-start(bf16[32,3712]{1,0:T(8,128)(2,1)S(1)} %collective-permute-done.8.refs_8_), channel_id=1, source_target_pairs={{0,2},{2,4},{4,6},{6,8},{8,10},{10,12},{12,14},{14,0},{1,15},{3,1}... | collective-permute-start | bytes 712712 | tf_op jit(solution)/shard_map/ppermute | solution.py:228
  28.6 2.2 %collective-permute-start.9 = (bf16[32,3712]{1,0:T(8,128)(2,1)S(1)}, bf16[32,3712]{1,0:T(8,128)(2,1)S(1)}, u32[]{:S(2)}, u32[]{:S(2)}) collective-permute-start(bf16[32,3712]{1,0:T(8,128)(2,1)S(1)} %collective-permute-done.8.refs_8_), channel_id=1, source_target_pairs={{0,16},{16,128},{128,144},{144,0},{1,145},{17,1},{129,17},{145,129... | collective-permute-start | bytes 712712 | tf_op jit(solution)/shard_map/ppermute | solution.py:228
  30.8 1.1 %collective-permute-start.14 = (bf16[32,3712]{1,0:T(8,128)(2,1)S(1)}, bf16[32,3712]{1,0:T(8,128)(2,1)S(1)}, u32[]{:S(2)}, u32[]{:S(2)}) collective-permute-start(bf16[32,3712]{1,0:T(8,128)(2,1)S(1)} %collective-permute-done.10.refs_10_), channel_id=1, source_target_pairs={{0,2},{2,4},{4,6},{6,8},{8,10},{10,12},{12,14},{14,0},{1,15},{3,1}... | collective-permute-start | bytes 712712 | tf_op jit(solution)/shard_map/ppermute | solution.py:228
  32.0 2.5 %collective-permute-start.7 = (bf16[32,3712]{1,0:T(8,128)(2,1)S(1)}, bf16[32,3712]{1,0:T(8,128)(2,1)S(1)}, u32[]{:S(2)}, u32[]{:S(2)}) collective-permute-start(bf16[32,3712]{1,0:T(8,128)(2,1)S(1)} %collective-permute-done.6.refs_6_), channel_id=1, source_target_pairs={{0,16},{16,128},{128,144},{144,0},{1,145},{17,1},{129,17},{145,129... | collective-permute-start | bytes 712712 | tf_op jit(solution)/shard_map/ppermute | solution.py:228
  34.4 2.3 %collective-permute-start.16 = (bf16[32,3712]{1,0:T(8,128)(2,1)S(1)}, bf16[32,3712]{1,0:T(8,128)(2,1)S(1)}, u32[]{:S(2)}, u32[]{:S(2)}) collective-permute-start(bf16[32,3712]{1,0:T(8,128)(2,1)S(1)} %collective-permute-done.12.refs_12_), channel_id=1, source_target_pairs={{1,15},{3,1},{5,3},{7,5},{9,7},{11,9},{13,11},{15,13},{17,31},{19,... | collective-permute-start | bytes 712712 | tf_op jit(solution)/shard_map/ppermute | solution.py:228
  36.7 2.3 %collective-permute-start.13 = (bf16[32,3712]{1,0:T(8,128)(2,1)S(1)}, bf16[32,3712]{1,0:T(8,128)(2,1)S(1)}, u32[]{:S(2)}, u32[]{:S(2)}) collective-permute-start(bf16[32,3712]{1,0:T(8,128)(2,1)S(1)} %collective-permute-done.12.refs_12_), channel_id=1, source_target_pairs={{0,16},{16,128},{128,144},{144,0},{1,145},{17,1},{129,17},{145,129... | collective-permute-start | bytes 712712 | tf_op jit(solution)/shard_map/ppermute | solution.py:228
  39.0 1.9 %collective-permute-start.18 = (bf16[32,3712]{1,0:T(8,128)(2,1)S(1)}, bf16[32,3712]{1,0:T(8,128)(2,1)}, u32[]{:S(2)}, u32[]{:S(2)}) collective-permute-start(bf16[32,3712]{1,0:T(8,128)(2,1)S(1)} %collective-permute-done.14.refs_14_), channel_id=1, source_target_pairs={{1,15},{3,1},{5,3},{7,5},{9,7},{11,9},{13,11},{15,13},{17,31},{19,... | collective-permute-start | bytes 712712 | tf_op jit(solution)/shard_map/ppermute | solution.py:228
  40.9 1.7 %collective-permute-start.11 = (bf16[32,3712]{1,0:T(8,128)(2,1)S(1)}, bf16[32,3712]{1,0:T(8,128)(2,1)}, u32[]{:S(2)}, u32[]{:S(2)}) collective-permute-start(bf16[32,3712]{1,0:T(8,128)(2,1)S(1)} %collective-permute-done.10.refs_10_), channel_id=1, source_target_pairs={{0,16},{16,128},{128,144},{144,0},{1,145},{17,1},{129,17},{145,129... | collective-permute-start | bytes 712712 | tf_op jit(solution)/shard_map/ppermute | solution.py:228
  42.6 0.5 collective-permute-start.15
  43.2 3.9 %collective-permute-start.17 = (bf16[32,3712]{1,0:T(8,128)(2,1)S(1)}, bf16[32,3712]{1,0:T(8,128)(2,1)}, u32[]{:S(2)}, u32[]{:S(2)}) collective-permute-start(bf16[32,3712]{1,0:T(8,128)(2,1)S(1)} %collective-permute-done.16.refs_16_), channel_id=1, source_target_pairs={{1,145},{17,1},{129,17},{145,129},{3,147},{19,3},{131,19},{147,131... | collective-permute-start | bytes 712712 | tf_op jit(solution)/shard_map/ppermute | solution.py:228
  47.1 1.9 %collective-permute-start.19 = (bf16[32,3712]{1,0:T(8,128)(2,1)}, bf16[32,3712]{1,0:T(8,128)(2,1)}, u32[]{:S(2)}, u32[]{:S(2)}) collective-permute-start(bf16[32,3712]{1,0:T(8,128)(2,1)} %collective-permute-done.18.refs_18_), channel_id=1, source_target_pairs={{1,145},{17,1},{129,17},{145,129},{3,147},{19,3},{131,19},{147,131... | collective-permute-start | bytes 712712 | tf_op jit(solution)/shard_map/ppermute | solution.py:228
  49.0 0.7 compare_select_fusion.6.index_ref
  49.7 1.7 %collective-permute-done.17.refs_17_ = bf16[32,3712]{1,0:T(8,128)(2,1)} collective-permute-done((bf16[32,3712]{1,0:T(8,128)(2,1)S(1)}, bf16[32,3712]{1,0:T(8,128)(2,1)}, u32[]{:S(2)}, u32[]{:S(2)}) %collective-permute-start.17) | collective-permute-done | bytes 237600 | tf_op jit(solution)/shard_map/ppermute | solution.py:228
  51.4 2.8 %collective-permute-done.19.refs_19_ = bf16[32,3712]{1,0:T(8,128)(2,1)} collective-permute-done((bf16[32,3712]{1,0:T(8,128)(2,1)}, bf16[32,3712]{1,0:T(8,128)(2,1)}, u32[]{:S(2)}, u32[]{:S(2)}) %collective-permute-start.19) | collective-permute-done | bytes 237600 | tf_op jit(solution)/shard_map/ppermute | solution.py:228
  54.2 0.9 copy-done
  55.2 13.2 %score.1 = (f32[16,1,1024]{2,1,0:T(1,128)S(1)}, f32[2,512]{1,0:T(2,128)S(1)}) custom-call(s32[25]{0:T(128)S(1)} %compare_select_fusion.6.index_ref, bf16[3584,1024]{1,0:T(8,128)(2,1)} %a_ref.1, bf16[3584,1024]{1,0:T(8,128)(2,1)} %collective-permute-done.b_ref, bf16[32,3712]{1,0:T(8,128)(2,1)S(1)} %copy-done, ...), custom_call_target="tpu_custom_call" | custom-call | flops 7516192768 | bytes 14680064 | tf_op jit(solution)/shard_map/score/pallas_call | solution.py:254
  68.4 12.6 %all_to_all.10.parts_ref = f32[16,1,1024]{2,1,0:T(1,128)S(1)} all-to-all(f32[16,1,1024]{2,1,0:T(1,128)S(1)} %get-tuple-element.6), channel_id=1, replica_groups=mesh['xh'=2,'y'=4,'xl'=2,'z'=8,'c'=2] {'xh','xl','y'}, dimensions={0} | all-to-all | bytes 131072 | tf_op jit(solution)/shard_map/all_to_all | solution.py:32
  81.1 13.7 %all_to_all.11.parts_ref = f32[16,1,2048]{2,1,0:T(1,128)S(1)} all-to-all(f32[16,1,2048]{2,1,0:T(1,128)S(1)} %merge.1), channel_id=1, replica_groups=mesh['xh'=2,'y'=4,'xl'=2,'z'=8,'c'=2] {'z','c'}, dimensions={0} | all-to-all | bytes 262144 | tf_op jit(solution)/shard_map/all_to_all | solution.py:32
  94.8 1.5 %finish.1 = (f32[1,128]{1,0:T(1,128)S(1)}, f32[1,512]{1,0:T(1,128)}) custom-call(s32[25]{0:T(128)S(1)} %compare_select_fusion.6.index_ref, f32[16,1,2048]{2,1,0:T(1,128)S(1)} %all_to_all.11.parts_ref), custom_call_target="tpu_custom_call" | custom-call | tf_op jit(solution)/shard_map/finish/pallas_call | solution.py:283
  96.3 0.5 slice_bitcast_fusion
  (18 shorter events, 0.1 us)
Async XLA Ops:
  0.6 53.6 %collective-permute-start = (bf16[3584,1024]{1,0:T(8,128)(2,1)}, bf16[3584,1024]{1,0:T(8,128)(2,1)}, u32[]{:S(2)}, u32[]{:S(2)}) collective-permute-start(bf16[3584,1024]{1,0:T(8,128)(2,1)} %a_ref.1), channel_id=1, source_target_pairs={{0,1},{1,0},{2,3},{3,2},{4,5},{5,4},{6,7},{7,6},{8,9},{9,8},{10,11... | collective-permute-start | bytes 22020104 | tf_op jit(solution)/shard_map/ppermute | solution.py:28
  5.6 10.1 %collective-permute-start.2 = (bf16[32,3712]{1,0:T(8,128)(2,1)}, bf16[32,3712]{1,0:T(8,128)(2,1)S(1)}, u32[]{:S(2)}, u32[]{:S(2)}) collective-permute-start(bf16[32,3712]{1,0:T(8,128)(2,1)} %tag.1.refs_0_), channel_id=1, source_target_pairs={{0,1},{1,0},{2,3},{3,2},{4,5},{5,4},{6,7},{7,6},{8,9},{9,8},{10,11... | collective-permute-start | bytes 712712 | tf_op jit(solution)/shard_map/ppermute | solution.py:28
  5.8 14.5 %collective-permute-start.4 = (bf16[32,3712]{1,0:T(8,128)(2,1)}, bf16[32,3712]{1,0:T(8,128)(2,1)S(1)}, u32[]{:S(2)}, u32[]{:S(2)}) collective-permute-start(bf16[32,3712]{1,0:T(8,128)(2,1)} %tag.1.refs_0_), channel_id=1, source_target_pairs={{0,2},{2,4},{4,6},{6,8},{8,10},{10,12},{12,14},{14,0},{1,15},{3,1}... | collective-permute-start | bytes 712712 | tf_op jit(solution)/shard_map/ppermute | solution.py:228
  15.8 7.8 %collective-permute-start.6 = (bf16[32,3712]{1,0:T(8,128)(2,1)S(1)}, bf16[32,3712]{1,0:T(8,128)(2,1)S(1)}, u32[]{:S(2)}, u32[]{:S(2)}) collective-permute-start(bf16[32,3712]{1,0:T(8,128)(2,1)S(1)} %collective-permute-done.2.refs_2_), channel_id=1, source_target_pairs={{0,2},{2,4},{4,6},{6,8},{8,10},{10,12},{12,14},{14,0},{1,15},{3,1}... | collective-permute-start | bytes 712712 | tf_op jit(solution)/shard_map/ppermute | solution.py:228
  19.6 6.2 %collective-permute-start.1 = (bf16[32,3712]{1,0:T(8,128)(2,1)}, bf16[32,3712]{1,0:T(8,128)(2,1)S(1)}, u32[]{:S(2)}, u32[]{:S(2)}) collective-permute-start(bf16[32,3712]{1,0:T(8,128)(2,1)} %tag.1.refs_0_), channel_id=1, source_target_pairs={{0,16},{16,128},{128,144},{144,0},{2,18},{18,130},{130,146},{146,2... | collective-permute-start | bytes 712712 | tf_op jit(solution)/shard_map/ppermute | solution.py:228
  20.3 6.2 %collective-permute-start.8 = (bf16[32,3712]{1,0:T(8,128)(2,1)S(1)}, bf16[32,3712]{1,0:T(8,128)(2,1)S(1)}, u32[]{:S(2)}, u32[]{:S(2)}) collective-permute-start(bf16[32,3712]{1,0:T(8,128)(2,1)S(1)} %collective-permute-done.4.refs_4_), channel_id=1, source_target_pairs={{0,2},{2,4},{4,6},{6,8},{8,10},{10,12},{12,14},{14,0},{1,15},{3,1}... | collective-permute-start | bytes 712712 | tf_op jit(solution)/shard_map/ppermute | solution.py:228
  21.1 7.5 %collective-permute-start.5 = (bf16[32,3712]{1,0:T(8,128)(2,1)S(1)}, bf16[32,3712]{1,0:T(8,128)(2,1)S(1)}, u32[]{:S(2)}, u32[]{:S(2)}) collective-permute-start(bf16[32,3712]{1,0:T(8,128)(2,1)S(1)} %collective-permute-done.4.refs_4_), channel_id=1, source_target_pairs={{0,16},{16,128},{128,144},{144,0},{1,145},{17,1},{129,17},{145,129... | collective-permute-start | bytes 712712 | tf_op jit(solution)/shard_map/ppermute | solution.py:228
  23.6 7.2 %collective-permute-start.10 = (bf16[32,3712]{1,0:T(8,128)(2,1)S(1)}, bf16[32,3712]{1,0:T(8,128)(2,1)S(1)}, u32[]{:S(2)}, u32[]{:S(2)}) collective-permute-start(bf16[32,3712]{1,0:T(8,128)(2,1)S(1)} %collective-permute-done.6.refs_6_), channel_id=1, source_target_pairs={{0,2},{2,4},{4,6},{6,8},{8,10},{10,12},{12,14},{14,0},{1,15},{3,1}... | collective-permute-start | bytes 712712 | tf_op jit(solution)/shard_map/ppermute | solution.py:228
  25.8 6.2 %collective-permute-start.3 = (bf16[32,3712]{1,0:T(8,128)(2,1)S(1)}, bf16[32,3712]{1,0:T(8,128)(2,1)S(1)}, u32[]{:S(2)}, u32[]{:S(2)}) collective-permute-start(bf16[32,3712]{1,0:T(8,128)(2,1)S(1)} %collective-permute-done.2.refs_2_), channel_id=1, source_target_pairs={{0,16},{16,128},{128,144},{144,0},{2,18},{18,130},{130,146},{146,2... | collective-permute-start | bytes 712712 | tf_op jit(solution)/shard_map/ppermute | solution.py:228
  26.5 8.0 %collective-permute-start.12 = (bf16[32,3712]{1,0:T(8,128)(2,1)S(1)}, bf16[32,3712]{1,0:T(8,128)(2,1)S(1)}, u32[]{:S(2)}, u32[]{:S(2)}) collective-permute-start(bf16[32,3712]{1,0:T(8,128)(2,1)S(1)} %collective-permute-done.8.refs_8_), channel_id=1, source_target_pairs={{0,2},{2,4},{4,6},{6,8},{8,10},{10,12},{12,14},{14,0},{1,15},{3,1}... | collective-permute-start | bytes 712712 | tf_op jit(solution)/shard_map/ppermute | solution.py:228
  28.6 8.1 %collective-permute-start.9 = (bf16[32,3712]{1,0:T(8,128)(2,1)S(1)}, bf16[32,3712]{1,0:T(8,128)(2,1)S(1)}, u32[]{:S(2)}, u32[]{:S(2)}) collective-permute-start(bf16[32,3712]{1,0:T(8,128)(2,1)S(1)} %collective-permute-done.8.refs_8_), channel_id=1, source_target_pairs={{0,16},{16,128},{128,144},{144,0},{1,145},{17,1},{129,17},{145,129... | collective-permute-start | bytes 712712 | tf_op jit(solution)/shard_map/ppermute | solution.py:228
  30.8 8.2 %collective-permute-start.14 = (bf16[32,3712]{1,0:T(8,128)(2,1)S(1)}, bf16[32,3712]{1,0:T(8,128)(2,1)S(1)}, u32[]{:S(2)}, u32[]{:S(2)}) collective-permute-start(bf16[32,3712]{1,0:T(8,128)(2,1)S(1)} %collective-permute-done.10.refs_10_), channel_id=1, source_target_pairs={{0,2},{2,4},{4,6},{6,8},{8,10},{10,12},{12,14},{14,0},{1,15},{3,1}... | collective-permute-start | bytes 712712 | tf_op jit(solution)/shard_map/ppermute | solution.py:228
  32.0 8.9 %collective-permute-start.7 = (bf16[32,3712]{1,0:T(8,128)(2,1)S(1)}, bf16[32,3712]{1,0:T(8,128)(2,1)S(1)}, u32[]{:S(2)}, u32[]{:S(2)}) collective-permute-start(bf16[32,3712]{1,0:T(8,128)(2,1)S(1)} %collective-permute-done.6.refs_6_), channel_id=1, source_target_pairs={{0,16},{16,128},{128,144},{144,0},{1,145},{17,1},{129,17},{145,129... | collective-permute-start | bytes 712712 | tf_op jit(solution)/shard_map/ppermute | solution.py:228
  34.4 8.2 %collective-permute-start.16 = (bf16[32,3712]{1,0:T(8,128)(2,1)S(1)}, bf16[32,3712]{1,0:T(8,128)(2,1)S(1)}, u32[]{:S(2)}, u32[]{:S(2)}) collective-permute-start(bf16[32,3712]{1,0:T(8,128)(2,1)S(1)} %collective-permute-done.12.refs_12_), channel_id=1, source_target_pairs={{1,15},{3,1},{5,3},{7,5},{9,7},{11,9},{13,11},{15,13},{17,31},{19,... | collective-permute-start | bytes 712712 | tf_op jit(solution)/shard_map/ppermute | solution.py:228
  36.7 6.4 %collective-permute-start.13 = (bf16[32,3712]{1,0:T(8,128)(2,1)S(1)}, bf16[32,3712]{1,0:T(8,128)(2,1)S(1)}, u32[]{:S(2)}, u32[]{:S(2)}) collective-permute-start(bf16[32,3712]{1,0:T(8,128)(2,1)S(1)} %collective-permute-done.12.refs_12_), channel_id=1, source_target_pairs={{0,16},{16,128},{128,144},{144,0},{1,145},{17,1},{129,17},{145,129... | collective-permute-start | bytes 712712 | tf_op jit(solution)/shard_map/ppermute | solution.py:228
  39.0 8.1 %collective-permute-start.18 = (bf16[32,3712]{1,0:T(8,128)(2,1)S(1)}, bf16[32,3712]{1,0:T(8,128)(2,1)}, u32[]{:S(2)}, u32[]{:S(2)}) collective-permute-start(bf16[32,3712]{1,0:T(8,128)(2,1)S(1)} %collective-permute-done.14.refs_14_), channel_id=1, source_target_pairs={{1,15},{3,1},{5,3},{7,5},{9,7},{11,9},{13,11},{15,13},{17,31},{19,... | collective-permute-start | bytes 712712 | tf_op jit(solution)/shard_map/ppermute | solution.py:228
  40.9 8.8 %collective-permute-start.11 = (bf16[32,3712]{1,0:T(8,128)(2,1)S(1)}, bf16[32,3712]{1,0:T(8,128)(2,1)}, u32[]{:S(2)}, u32[]{:S(2)}) collective-permute-start(bf16[32,3712]{1,0:T(8,128)(2,1)S(1)} %collective-permute-done.10.refs_10_), channel_id=1, source_target_pairs={{0,16},{16,128},{128,144},{144,0},{1,145},{17,1},{129,17},{145,129... | collective-permute-start | bytes 712712 | tf_op jit(solution)/shard_map/ppermute | solution.py:228
  42.6 8.8 %collective-permute-start.15 = (bf16[32,3712]{1,0:T(8,128)(2,1)S(1)}, bf16[32,3712]{1,0:T(8,128)(2,1)}, u32[]{:S(2)}, u32[]{:S(2)}) collective-permute-start(bf16[32,3712]{1,0:T(8,128)(2,1)S(1)} %collective-permute-done.14.refs_14_), channel_id=1, source_target_pairs={{0,16},{16,128},{128,144},{144,0},{1,145},{17,1},{129,17},{145,129... | collective-permute-start | bytes 712712 | tf_op jit(solution)/shard_map/ppermute | solution.py:228
  43.2 8.3 %collective-permute-start.17 = (bf16[32,3712]{1,0:T(8,128)(2,1)S(1)}, bf16[32,3712]{1,0:T(8,128)(2,1)}, u32[]{:S(2)}, u32[]{:S(2)}) collective-permute-start(bf16[32,3712]{1,0:T(8,128)(2,1)S(1)} %collective-permute-done.16.refs_16_), channel_id=1, source_target_pairs={{1,145},{17,1},{129,17},{145,129},{3,147},{19,3},{131,19},{147,131... | collective-permute-start | bytes 712712 | tf_op jit(solution)/shard_map/ppermute | solution.py:228
  47.1 7.2 %collective-permute-start.19 = (bf16[32,3712]{1,0:T(8,128)(2,1)}, bf16[32,3712]{1,0:T(8,128)(2,1)}, u32[]{:S(2)}, u32[]{:S(2)}) collective-permute-start(bf16[32,3712]{1,0:T(8,128)(2,1)} %collective-permute-done.18.refs_18_), channel_id=1, source_target_pairs={{1,145},{17,1},{129,17},{145,129},{3,147},{19,3},{131,19},{147,131... | collective-permute-start | bytes 712712 | tf_op jit(solution)/shard_map/ppermute | solution.py:228
  54.2 0.9 copy-start

commit v2 on v1

--- a/solution.py
+++ b/solution.py
@@ -14,9 +14,9 @@
 X = ("xh", "xl")
 PLANE = ("xh", "xl", "y")
 LANES = 128
-TILE = 256
+TILE = 512
 VMEM_BYTES = 67043328
-HEADER = 5
+HEADER = 6
 
 VMEM = pl.BlockSpec(memory_space=pltpu.VMEM)
 SMEM = pl.BlockSpec(memory_space=pltpu.SMEM)
@@ -64,9 +64,11 @@
     rows, depth = x_ref.shape[0], a_ref.shape[0]
     per_head = a_ref.shape[1] // TILE
     count = 2 * per_head
+    copies = []
     for j in range(count):
         source = (a_ref, b_ref)[j // per_head].at[:, pl.ds(j % per_head * TILE, TILE)]
-        pltpu.make_async_copy(source, tiles.at[j], sems.at[j]).start()
+        copies.append(pltpu.make_async_copy(source, tiles.at[j], sems.at[j]))
+        copies[j].start()
     peak[...] = jnp.full(peak.shape, -jnp.inf, jnp.float32)
 
     def take(some):
@@ -79,17 +81,14 @@
     pl.when(index_ref[2] == 0)(lambda: take(first))
     pl.when(index_ref[2] != 0)(lambda: take(last))
 
-    def multiply(j, carry):
-        pltpu.make_async_copy(a_ref.at[:, pl.ds(0, TILE)], tiles.at[j], sems.at[j]).wait()
+    for j, copy in enumerate(copies):
+        copy.wait()
         part = jnp.dot(x_ref[:, :depth], tiles[j], preferred_element_type=jnp.float32)
         logits[j] = part
         top = peak[...]
         for h in range(TILE // LANES):
             top = jnp.maximum(top, part[:, h * LANES : (h + 1) * LANES])
         peak[...] = top
-        return carry
-
-    lax.fori_loop(0, count, multiply, 0)
 
     lane = lax.broadcasted_iota(jnp.int32, (1, LANES), 1).astype(jnp.float32)
 
@@ -135,12 +134,25 @@
     return lse, sum(parts_ref[k, :, rows:] for k in range(n))
 
 
-def merge_kernel(parts_ref, meta_ref, out_ref):
+def merge_kernel(index_ref, parts_ref, meta_ref, out_ref, *, half):
     lse, picked = merged(parts_ref)
     rows = lse.shape[1]
+    lane = lax.broadcasted_iota(jnp.int32, (1, rows), 1)
+    span = rows // (2 * half)
+    slot = lax.rem(lax.div(lane, span), half)
+    mine = (slot == index_ref[5]) & (index_ref[2] == 0)
+    picked = picked + jnp.where(mine, meta_ref[1:2, :], 0.0)
+    seq = jnp.where(mine, meta_ref[0:1, :], 0.0)
+    low = jnp.where(lane < rows // 2, seq, 0.0)
+    high = jnp.where(lane < rows // 2, 0.0, seq)
+    shift = index_ref[5] * span
+    low = pltpu.roll(low, lax.rem(rows - shift, rows), 1)
+    high = pltpu.roll(high, lax.rem(rows // 2 + rows - shift + span, rows), 1)
+    ids = (low + high)[:, :LANES]
     for k in range(out_ref.shape[0]):
-        for i, value in enumerate((lse, picked, meta_ref[0:1, :], meta_ref[1:2, :])):
-            out_ref[k, :, i * rows : (i + 1) * rows] = value
+        out_ref[k, :, :rows] = lse
+        out_ref[k, :, rows : 2 * rows] = picked
+        out_ref[k, :, 2 * rows :] = ids
 
 
 def held(z, c, nz):
@@ -149,7 +161,7 @@
 
 
 def finish_kernel(index_ref, parts_ref, own_ref, score_ref, *, nz, span):
-    rows, count, half = parts_ref.shape[2] // 4, score_ref.shape[1], nz // 2
+    rows, count, half = (parts_ref.shape[2] - LANES) // 2, score_ref.shape[1], nz // 2
     lane = lax.broadcasted_iota(jnp.int32, (1, rows), 1)
     slot = lax.rem(lax.div(lane, span), half)
 
@@ -159,7 +171,7 @@
     excesses, sums = [], None
     for low in (True, False):
         lses, picked = [], jnp.zeros((1, rows), jnp.float32)
-        seq, loss = jnp.zeros((1, rows), jnp.float32), jnp.zeros((1, rows), jnp.float32)
+        seq = jnp.zeros((1, rows), jnp.float32)
         for k in range(2 * nz):
             zs = [z for z in held(k // 2, k % 2, nz) if (z < half) == low]
             if not zs:
@@ -169,12 +181,15 @@
             picked += jnp.where(here, field(k, 1), 0.0)
         for z in range(nz):
             if (z < half) == low:
-                here = slot == z % half
-                seq = jnp.where(here, field(2 * z, 2), seq)
-                loss = jnp.where(here, field(2 * z, 3), loss)
+                ids = jnp.concatenate([parts_ref[2 * z, :, 2 * rows :]] + [jnp.zeros((1, LANES), jnp.float32)] * (rows // LANES - 1), axis=1)
+                even = jnp.where(lane < span, ids, 0.0)
+                shift = z % half * span
+                even = pltpu.roll(even, shift, 1) if shift else even
+                odd = jnp.where(lane < span, 0.0, ids)
+                seq += even + pltpu.roll(odd, rows // 2 - span + shift, 1)
         highest = functools.reduce(jnp.maximum, lses)
         lse = highest + jnp.log(sum(jnp.exp(l - highest) for l in lses))
-        excess = lse - picked - loss
+        excess = lse - picked
         excesses.append(excess)
         ids = lax.broadcasted_iota(jnp.int32, (count, rows), 0).astype(jnp.float32)
         member = jnp.where(ids == seq, 1.0, 0.0).astype(jnp.bfloat16)
@@ -245,7 +260,7 @@
     span = 2 * local
     slot = lax.rem(z + jnp.where(c == 0, nz - steps, steps), half)
     index = ((xl ^ other) * half + slot) * span + (c ^ piece) * local
-    fixed = ((block + c) * width, (block + 1 - c) * width, c, (xl * half + z % half) * span + c * local, z // half)
+    fixed = ((block + c) * width, (block + 1 - c) * width, c, (xl * half + z % half) * span + c * local, z // half, z % half)
     for i, value in enumerate(fixed):
         index = jnp.where(k == i, value, index)
     tokens = 2 * nz * local
@@ -273,13 +288,13 @@
         name="score",
     )(index, head, partner_head, *blocks)
     stats = pl.pallas_call(
-        merge_kernel,
-        out_shape=jax.ShapeDtypeStruct((2 * nz, 1, 4 * tokens), jnp.float32),
-        in_specs=[VMEM, VMEM],
+        functools.partial(merge_kernel, half=half),
+        out_shape=jax.ShapeDtypeStruct((2 * nz, 1, 2 * tokens + LANES), jnp.float32),
+        in_specs=[SMEM, VMEM, VMEM],
         out_specs=VMEM,
         compiler_params=pltpu.CompilerParams(vmem_limit_bytes=2 << 20),
         name="merge",
-    )(exchange(stats, PLANE), meta)
+    )(index, exchange(stats, PLANE), meta)
     own, score = pl.pallas_call(
         functools.partial(finish_kernel, nz=nz, span=span),
         out_shape=(

time: 97.2 us -> 96.7 us (level)
  no operation moved by 1% of the time
where the time goes in v2:
time: 96.7 us; the launch traced here: 96.3 us
  starting transfers between devices  40.4 us (42%)
  blocking collectives  25.4 us (26%)
  Pallas kernels  16.9 us (17%)
  waiting for transfers between devices  10.6 us (11%)
  local copies, waits for them, and re-layouts  1.45 us (1%)
    ppermute x18, starting transfers between devices, along(): return lax.ppermute(value, axes, pairs)  37 us
    all_to_all x2, blocking collectives, exchange(): return lax.all_to_all(copies, axis, 0, 0, tiled=True)  25.4 us
    pallas_call x1, Pallas kernels, on_device(): pl.pallas_call(score_kernel, out_shape=(jax.ShapeDtypeStruct((plane, 1, 2...  13 us
    ppermute x2, waiting for transfers between devices, hop(): return lax.ppermute(value, axis, [(i, (i + step) % n) for i in range(n)])  6.07 us
    ppermute x18, waiting for transfers between devices, along(): return lax.ppermute(value, axes, pairs)  4.52 us
    ppermute x2, starting transfers between devices, hop(): return lax.ppermute(value, axis, [(i, (i + step) % n) for i in range(n)])  3.39 us
  transfers between devices with their start and end apart: 20, of which 3 were waited for; matrix products, arithmetic and copies ran while one was open for 1% of the time, Pallas kernels for 2%

profile of v2, /device:TPU:1, one launch (start us, length us, event | category | flops | bytes accessed | tf_op | source)
XLA Modules:
  0.0 96.3 jit_solution(1313651040127574405)
XLA Ops:
  0.6 3.3 %collective-permute-start = (bf16[3584,1024]{1,0:T(8,128)(2,1)}, bf16[3584,1024]{1,0:T(8,128)(2,1)}, u32[]{:S(2)}, u32[]{:S(2)}) collective-permute-start(bf16[3584,1024]{1,0:T(8,128)(2,1)} %a_ref.1), channel_id=1, source_target_pairs={{0,1},{1,0},{2,3},{3,2},{4,5},{5,4},{6,7},{7,6},{8,9},{9,8},{10,11... | collective-permute-start | bytes 22020104 | tf_op jit(solution)/shard_map/ppermute | solution.py:28
  3.9 1.7 %tag.1.refs_0_ = bf16[32,3712]{1,0:T(8,128)(2,1)} custom-call(bf16[32,3584]{1,0:T(8,128)(2,1)} %states_in.1, s32[1,32]{1,0:T(1,128)} %bitcast.14, f32[1,32]{1,0:T(1,128)} %bitcast.15, s32[1,32]{1,0:T(1,128)} %bitcast.16), custom_call_target="tpu_custom_call" | custom-call | tf_op jit(solution)/shard_map/tag/pallas_call | solution.py:219
  5.6 0.1 collective-permute-start.2
  5.8 3.9 %collective-permute-start.4 = (bf16[32,3712]{1,0:T(8,128)(2,1)}, bf16[32,3712]{1,0:T(8,128)(2,1)S(1)}, u32[]{:S(2)}, u32[]{:S(2)}) collective-permute-start(bf16[32,3712]{1,0:T(8,128)(2,1)} %tag.1.refs_0_), channel_id=1, source_target_pairs={{0,2},{2,4},{4,6},{6,8},{8,10},{10,12},{12,14},{14,0},{1,15},{3,1}... | collective-permute-start | bytes 712712 | tf_op jit(solution)/shard_map/ppermute | solution.py:243
  9.7 6.1 %collective-permute-done.2.refs_2_ = bf16[32,3712]{1,0:T(8,128)(2,1)S(1)} collective-permute-done((bf16[32,3712]{1,0:T(8,128)(2,1)}, bf16[32,3712]{1,0:T(8,128)(2,1)S(1)}, u32[]{:S(2)}, u32[]{:S(2)}) %collective-permute-start.2) | collective-permute-done | bytes 237600 | tf_op jit(solution)/shard_map/ppermute | solution.py:28
  15.8 3.9 %collective-permute-start.6 = (bf16[32,3712]{1,0:T(8,128)(2,1)S(1)}, bf16[32,3712]{1,0:T(8,128)(2,1)S(1)}, u32[]{:S(2)}, u32[]{:S(2)}) collective-permute-start(bf16[32,3712]{1,0:T(8,128)(2,1)S(1)} %collective-permute-done.2.refs_2_), channel_id=1, source_target_pairs={{0,2},{2,4},{4,6},{6,8},{8,10},{10,12},{12,14},{14,0},{1,15},{3,1}... | collective-permute-start | bytes 712712 | tf_op jit(solution)/shard_map/ppermute | solution.py:243
  19.6 0.7 collective-permute-start.1
  20.3 0.8 collective-permute-start.8
  21.1 2.5 %collective-permute-start.5 = (bf16[32,3712]{1,0:T(8,128)(2,1)S(1)}, bf16[32,3712]{1,0:T(8,128)(2,1)S(1)}, u32[]{:S(2)}, u32[]{:S(2)}) collective-permute-start(bf16[32,3712]{1,0:T(8,128)(2,1)S(1)} %collective-permute-done.4.refs_4_), channel_id=1, source_target_pairs={{0,16},{16,128},{128,144},{144,0},{1,145},{17,1},{129,17},{145,129... | collective-permute-start | bytes 712712 | tf_op jit(solution)/shard_map/ppermute | solution.py:243
  23.6 2.2 %collective-permute-start.10 = (bf16[32,3712]{1,0:T(8,128)(2,1)S(1)}, bf16[32,3712]{1,0:T(8,128)(2,1)S(1)}, u32[]{:S(2)}, u32[]{:S(2)}) collective-permute-start(bf16[32,3712]{1,0:T(8,128)(2,1)S(1)} %collective-permute-done.6.refs_6_), channel_id=1, source_target_pairs={{0,2},{2,4},{4,6},{6,8},{8,10},{10,12},{12,14},{14,0},{1,15},{3,1}... | collective-permute-start | bytes 712712 | tf_op jit(solution)/shard_map/ppermute | solution.py:243
  25.8 0.7 collective-permute-start.3
  26.5 2.2 %collective-permute-start.12 = (bf16[32,3712]{1,0:T(8,128)(2,1)S(1)}, bf16[32,3712]{1,0:T(8,128)(2,1)S(1)}, u32[]{:S(2)}, u32[]{:S(2)}) collective-permute-start(bf16[32,3712]{1,0:T(8,128)(2,1)S(1)} %collective-permute-done.8.refs_8_), channel_id=1, source_target_pairs={{0,2},{2,4},{4,6},{6,8},{8,10},{10,12},{12,14},{14,0},{1,15},{3,1}... | collective-permute-start | bytes 712712 | tf_op jit(solution)/shard_map/ppermute | solution.py:243
  28.6 2.2 %collective-permute-start.9 = (bf16[32,3712]{1,0:T(8,128)(2,1)S(1)}, bf16[32,3712]{1,0:T(8,128)(2,1)S(1)}, u32[]{:S(2)}, u32[]{:S(2)}) collective-permute-start(bf16[32,3712]{1,0:T(8,128)(2,1)S(1)} %collective-permute-done.8.refs_8_), channel_id=1, source_target_pairs={{0,16},{16,128},{128,144},{144,0},{1,145},{17,1},{129,17},{145,129... | collective-permute-start | bytes 712712 | tf_op jit(solution)/shard_map/ppermute | solution.py:243
  30.8 1.1 %collective-permute-start.14 = (bf16[32,3712]{1,0:T(8,128)(2,1)S(1)}, bf16[32,3712]{1,0:T(8,128)(2,1)S(1)}, u32[]{:S(2)}, u32[]{:S(2)}) collective-permute-start(bf16[32,3712]{1,0:T(8,128)(2,1)S(1)} %collective-permute-done.10.refs_10_), channel_id=1, source_target_pairs={{0,2},{2,4},{4,6},{6,8},{8,10},{10,12},{12,14},{14,0},{1,15},{3,1}... | collective-permute-start | bytes 712712 | tf_op jit(solution)/shard_map/ppermute | solution.py:243
  32.0 2.5 %collective-permute-start.7 = (bf16[32,3712]{1,0:T(8,128)(2,1)S(1)}, bf16[32,3712]{1,0:T(8,128)(2,1)S(1)}, u32[]{:S(2)}, u32[]{:S(2)}) collective-permute-start(bf16[32,3712]{1,0:T(8,128)(2,1)S(1)} %collective-permute-done.6.refs_6_), channel_id=1, source_target_pairs={{0,16},{16,128},{128,144},{144,0},{1,145},{17,1},{129,17},{145,129... | collective-permute-start | bytes 712712 | tf_op jit(solution)/shard_map/ppermute | solution.py:243
  34.4 2.3 %collective-permute-start.16 = (bf16[32,3712]{1,0:T(8,128)(2,1)S(1)}, bf16[32,3712]{1,0:T(8,128)(2,1)S(1)}, u32[]{:S(2)}, u32[]{:S(2)}) collective-permute-start(bf16[32,3712]{1,0:T(8,128)(2,1)S(1)} %collective-permute-done.12.refs_12_), channel_id=1, source_target_pairs={{1,15},{3,1},{5,3},{7,5},{9,7},{11,9},{13,11},{15,13},{17,31},{19,... | collective-permute-start | bytes 712712 | tf_op jit(solution)/shard_map/ppermute | solution.py:243
  36.7 2.3 %collective-permute-start.13 = (bf16[32,3712]{1,0:T(8,128)(2,1)S(1)}, bf16[32,3712]{1,0:T(8,128)(2,1)S(1)}, u32[]{:S(2)}, u32[]{:S(2)}) collective-permute-start(bf16[32,3712]{1,0:T(8,128)(2,1)S(1)} %collective-permute-done.12.refs_12_), channel_id=1, source_target_pairs={{0,16},{16,128},{128,144},{144,0},{1,145},{17,1},{129,17},{145,129... | collective-permute-start | bytes 712712 | tf_op jit(solution)/shard_map/ppermute | solution.py:243
  39.0 1.9 %collective-permute-start.18 = (bf16[32,3712]{1,0:T(8,128)(2,1)S(1)}, bf16[32,3712]{1,0:T(8,128)(2,1)}, u32[]{:S(2)}, u32[]{:S(2)}) collective-permute-start(bf16[32,3712]{1,0:T(8,128)(2,1)S(1)} %collective-permute-done.14.refs_14_), channel_id=1, source_target_pairs={{1,15},{3,1},{5,3},{7,5},{9,7},{11,9},{13,11},{15,13},{17,31},{19,... | collective-permute-start | bytes 712712 | tf_op jit(solution)/shard_map/ppermute | solution.py:243
  40.9 1.7 %collective-permute-start.11 = (bf16[32,3712]{1,0:T(8,128)(2,1)S(1)}, bf16[32,3712]{1,0:T(8,128)(2,1)}, u32[]{:S(2)}, u32[]{:S(2)}) collective-permute-start(bf16[32,3712]{1,0:T(8,128)(2,1)S(1)} %collective-permute-done.10.refs_10_), channel_id=1, source_target_pairs={{0,16},{16,128},{128,144},{144,0},{1,145},{17,1},{129,17},{145,129... | collective-permute-start | bytes 712712 | tf_op jit(solution)/shard_map/ppermute | solution.py:243
  42.6 0.5 collective-permute-start.15
  43.2 3.9 %collective-permute-start.17 = (bf16[32,3712]{1,0:T(8,128)(2,1)S(1)}, bf16[32,3712]{1,0:T(8,128)(2,1)}, u32[]{:S(2)}, u32[]{:S(2)}) collective-permute-start(bf16[32,3712]{1,0:T(8,128)(2,1)S(1)} %collective-permute-done.16.refs_16_), channel_id=1, source_target_pairs={{1,145},{17,1},{129,17},{145,129},{3,147},{19,3},{131,19},{147,131... | collective-permute-start | bytes 712712 | tf_op jit(solution)/shard_map/ppermute | solution.py:243
  47.1 1.9 %collective-permute-start.19 = (bf16[32,3712]{1,0:T(8,128)(2,1)}, bf16[32,3712]{1,0:T(8,128)(2,1)}, u32[]{:S(2)}, u32[]{:S(2)}) collective-permute-start(bf16[32,3712]{1,0:T(8,128)(2,1)} %collective-permute-done.18.refs_18_), channel_id=1, source_target_pairs={{1,145},{17,1},{129,17},{145,129},{3,147},{19,3},{131,19},{147,131... | collective-permute-start | bytes 712712 | tf_op jit(solution)/shard_map/ppermute | solution.py:243
  49.0 0.7 compare_select_fusion.7.index_ref
  49.8 1.7 %collective-permute-done.17.refs_17_ = bf16[32,3712]{1,0:T(8,128)(2,1)} collective-permute-done((bf16[32,3712]{1,0:T(8,128)(2,1)S(1)}, bf16[32,3712]{1,0:T(8,128)(2,1)}, u32[]{:S(2)}, u32[]{:S(2)}) %collective-permute-start.17) | collective-permute-done | bytes 237600 | tf_op jit(solution)/shard_map/ppermute | solution.py:243
  51.4 2.8 %collective-permute-done.19.refs_19_ = bf16[32,3712]{1,0:T(8,128)(2,1)} collective-permute-done((bf16[32,3712]{1,0:T(8,128)(2,1)}, bf16[32,3712]{1,0:T(8,128)(2,1)}, u32[]{:S(2)}, u32[]{:S(2)}) %collective-permute-start.19) | collective-permute-done | bytes 237600 | tf_op jit(solution)/shard_map/ppermute | solution.py:243
  54.2 0.9 copy-done
  55.2 13.0 %score.1 = (f32[16,1,1024]{2,1,0:T(1,128)S(1)}, f32[2,512]{1,0:T(2,128)S(1)}) custom-call(s32[26]{0:T(128)S(1)} %compare_select_fusion.7.index_ref, bf16[3584,1024]{1,0:T(8,128)(2,1)} %a_ref.1, bf16[3584,1024]{1,0:T(8,128)(2,1)} %collective-permute-done.b_ref, bf16[32,3712]{1,0:T(8,128)(2,1)S(1)} %copy-done, ...), custom_call_target="tpu_custom_call" | custom-call | flops 7516192768 | bytes 14680064 | tf_op jit(solution)/shard_map/score/pallas_call | solution.py:269
  68.2 12.6 %all_to_all.10.parts_ref = f32[16,1,1024]{2,1,0:T(1,128)S(1)} all-to-all(f32[16,1,1024]{2,1,0:T(1,128)S(1)} %get-tuple-element.6), channel_id=1, replica_groups=mesh['xh'=2,'y'=4,'xl'=2,'z'=8,'c'=2] {'xh','xl','y'}, dimensions={0} | all-to-all | bytes 131072 | tf_op jit(solution)/shard_map/all_to_all | solution.py:32
  80.8 0.6 merge.1
  81.4 12.8 %all_to_all.11.parts_ref = f32[16,1,1152]{2,1,0:T(1,128)S(1)} all-to-all(f32[16,1,1152]{2,1,0:T(1,128)S(1)} %merge.1), channel_id=1, replica_groups=mesh['xh'=2,'y'=4,'xl'=2,'z'=8,'c'=2] {'z','c'}, dimensions={0} | all-to-all | bytes 147456 | tf_op jit(solution)/shard_map/all_to_all | solution.py:32
  94.2 1.6 %finish.1 = (f32[1,128]{1,0:T(1,128)S(1)}, f32[1,512]{1,0:T(1,128)}) custom-call(s32[26]{0:T(128)S(1)} %compare_select_fusion.7.index_ref, f32[16,1,1152]{2,1,0:T(1,128)S(1)} %all_to_all.11.parts_ref), custom_call_target="tpu_custom_call" | custom-call | tf_op jit(solution)/shard_map/finish/pallas_call | solution.py:298
  95.8 0.5 slice_bitcast_fusion
  (18 shorter events, 0.0 us)
Async XLA Ops:
  0.6 53.6 %collective-permute-start = (bf16[3584,1024]{1,0:T(8,128)(2,1)}, bf16[3584,1024]{1,0:T(8,128)(2,1)}, u32[]{:S(2)}, u32[]{:S(2)}) collective-permute-start(bf16[3584,1024]{1,0:T(8,128)(2,1)} %a_ref.1), channel_id=1, source_target_pairs={{0,1},{1,0},{2,3},{3,2},{4,5},{5,4},{6,7},{7,6},{8,9},{9,8},{10,11... | collective-permute-start | bytes 22020104 | tf_op jit(solution)/shard_map/ppermute | solution.py:28
  5.6 10.1 %collective-permute-start.2 = (bf16[32,3712]{1,0:T(8,128)(2,1)}, bf16[32,3712]{1,0:T(8,128)(2,1)S(1)}, u32[]{:S(2)}, u32[]{:S(2)}) collective-permute-start(bf16[32,3712]{1,0:T(8,128)(2,1)} %tag.1.refs_0_), channel_id=1, source_target_pairs={{0,1},{1,0},{2,3},{3,2},{4,5},{5,4},{6,7},{7,6},{8,9},{9,8},{10,11... | collective-permute-start | bytes 712712 | tf_op jit(solution)/shard_map/ppermute | solution.py:28
  5.8 14.5 %collective-permute-start.4 = (bf16[32,3712]{1,0:T(8,128)(2,1)}, bf16[32,3712]{1,0:T(8,128)(2,1)S(1)}, u32[]{:S(2)}, u32[]{:S(2)}) collective-permute-start(bf16[32,3712]{1,0:T(8,128)(2,1)} %tag.1.refs_0_), channel_id=1, source_target_pairs={{0,2},{2,4},{4,6},{6,8},{8,10},{10,12},{12,14},{14,0},{1,15},{3,1}... | collective-permute-start | bytes 712712 | tf_op jit(solution)/shard_map/ppermute | solution.py:243
  15.8 7.8 %collective-permute-start.6 = (bf16[32,3712]{1,0:T(8,128)(2,1)S(1)}, bf16[32,3712]{1,0:T(8,128)(2,1)S(1)}, u32[]{:S(2)}, u32[]{:S(2)}) collective-permute-start(bf16[32,3712]{1,0:T(8,128)(2,1)S(1)} %collective-permute-done.2.refs_2_), channel_id=1, source_target_pairs={{0,2},{2,4},{4,6},{6,8},{8,10},{10,12},{12,14},{14,0},{1,15},{3,1}... | collective-permute-start | bytes 712712 | tf_op jit(solution)/shard_map/ppermute | solution.py:243
  19.6 6.2 %collective-permute-start.1 = (bf16[32,3712]{1,0:T(8,128)(2,1)}, bf16[32,3712]{1,0:T(8,128)(2,1)S(1)}, u32[]{:S(2)}, u32[]{:S(2)}) collective-permute-start(bf16[32,3712]{1,0:T(8,128)(2,1)} %tag.1.refs_0_), channel_id=1, source_target_pairs={{0,16},{16,128},{128,144},{144,0},{2,18},{18,130},{130,146},{146,2... | collective-permute-start | bytes 712712 | tf_op jit(solution)/shard_map/ppermute | solution.py:243
  20.3 6.2 %collective-permute-start.8 = (bf16[32,3712]{1,0:T(8,128)(2,1)S(1)}, bf16[32,3712]{1,0:T(8,128)(2,1)S(1)}, u32[]{:S(2)}, u32[]{:S(2)}) collective-permute-start(bf16[32,3712]{1,0:T(8,128)(2,1)S(1)} %collective-permute-done.4.refs_4_), channel_id=1, source_target_pairs={{0,2},{2,4},{4,6},{6,8},{8,10},{10,12},{12,14},{14,0},{1,15},{3,1}... | collective-permute-start | bytes 712712 | tf_op jit(solution)/shard_map/ppermute | solution.py:243
  21.1 7.5 %collective-permute-start.5 = (bf16[32,3712]{1,0:T(8,128)(2,1)S(1)}, bf16[32,3712]{1,0:T(8,128)(2,1)S(1)}, u32[]{:S(2)}, u32[]{:S(2)}) collective-permute-start(bf16[32,3712]{1,0:T(8,128)(2,1)S(1)} %collective-permute-done.4.refs_4_), channel_id=1, source_target_pairs={{0,16},{16,128},{128,144},{144,0},{1,145},{17,1},{129,17},{145,129... | collective-permute-start | bytes 712712 | tf_op jit(solution)/shard_map/ppermute | solution.py:243
  23.6 7.2 %collective-permute-start.10 = (bf16[32,3712]{1,0:T(8,128)(2,1)S(1)}, bf16[32,3712]{1,0:T(8,128)(2,1)S(1)}, u32[]{:S(2)}, u32[]{:S(2)}) collective-permute-start(bf16[32,3712]{1,0:T(8,128)(2,1)S(1)} %collective-permute-done.6.refs_6_), channel_id=1, source_target_pairs={{0,2},{2,4},{4,6},{6,8},{8,10},{10,12},{12,14},{14,0},{1,15},{3,1}... | collective-permute-start | bytes 712712 | tf_op jit(solution)/shard_map/ppermute | solution.py:243
  25.8 6.2 %collective-permute-start.3 = (bf16[32,3712]{1,0:T(8,128)(2,1)S(1)}, bf16[32,3712]{1,0:T(8,128)(2,1)S(1)}, u32[]{:S(2)}, u32[]{:S(2)}) collective-permute-start(bf16[32,3712]{1,0:T(8,128)(2,1)S(1)} %collective-permute-done.2.refs_2_), channel_id=1, source_target_pairs={{0,16},{16,128},{128,144},{144,0},{2,18},{18,130},{130,146},{146,2... | collective-permute-start | bytes 712712 | tf_op jit(solution)/shard_map/ppermute | solution.py:243
  26.5 8.0 %collective-permute-start.12 = (bf16[32,3712]{1,0:T(8,128)(2,1)S(1)}, bf16[32,3712]{1,0:T(8,128)(2,1)S(1)}, u32[]{:S(2)}, u32[]{:S(2)}) collective-permute-start(bf16[32,3712]{1,0:T(8,128)(2,1)S(1)} %collective-permute-done.8.refs_8_), channel_id=1, source_target_pairs={{0,2},{2,4},{4,6},{6,8},{8,10},{10,12},{12,14},{14,0},{1,15},{3,1}... | collective-permute-start | bytes 712712 | tf_op jit(solution)/shard_map/ppermute | solution.py:243
  28.6 8.1 %collective-permute-start.9 = (bf16[32,3712]{1,0:T(8,128)(2,1)S(1)}, bf16[32,3712]{1,0:T(8,128)(2,1)S(1)}, u32[]{:S(2)}, u32[]{:S(2)}) collective-permute-start(bf16[32,3712]{1,0:T(8,128)(2,1)S(1)} %collective-permute-done.8.refs_8_), channel_id=1, source_target_pairs={{0,16},{16,128},{128,144},{144,0},{1,145},{17,1},{129,17},{145,129... | collective-permute-start | bytes 712712 | tf_op jit(solution)/shard_map/ppermute | solution.py:243
  30.8 8.2 %collective-permute-start.14 = (bf16[32,3712]{1,0:T(8,128)(2,1)S(1)}, bf16[32,3712]{1,0:T(8,128)(2,1)S(1)}, u32[]{:S(2)}, u32[]{:S(2)}) collective-permute-start(bf16[32,3712]{1,0:T(8,128)(2,1)S(1)} %collective-permute-done.10.refs_10_), channel_id=1, source_target_pairs={{0,2},{2,4},{4,6},{6,8},{8,10},{10,12},{12,14},{14,0},{1,15},{3,1}... | collective-permute-start | bytes 712712 | tf_op jit(solution)/shard_map/ppermute | solution.py:243
  32.0 8.9 %collective-permute-start.7 = (bf16[32,3712]{1,0:T(8,128)(2,1)S(1)}, bf16[32,3712]{1,0:T(8,128)(2,1)S(1)}, u32[]{:S(2)}, u32[]{:S(2)}) collective-permute-start(bf16[32,3712]{1,0:T(8,128)(2,1)S(1)} %collective-permute-done.6.refs_6_), channel_id=1, source_target_pairs={{0,16},{16,128},{128,144},{144,0},{1,145},{17,1},{129,17},{145,129... | collective-permute-start | bytes 712712 | tf_op jit(solution)/shard_map/ppermute | solution.py:243
  34.4 8.2 %collective-permute-start.16 = (bf16[32,3712]{1,0:T(8,128)(2,1)S(1)}, bf16[32,3712]{1,0:T(8,128)(2,1)S(1)}, u32[]{:S(2)}, u32[]{:S(2)}) collective-permute-start(bf16[32,3712]{1,0:T(8,128)(2,1)S(1)} %collective-permute-done.12.refs_12_), channel_id=1, source_target_pairs={{1,15},{3,1},{5,3},{7,5},{9,7},{11,9},{13,11},{15,13},{17,31},{19,... | collective-permute-start | bytes 712712 | tf_op jit(solution)/shard_map/ppermute | solution.py:243
  36.7 6.4 %collective-permute-start.13 = (bf16[32,3712]{1,0:T(8,128)(2,1)S(1)}, bf16[32,3712]{1,0:T(8,128)(2,1)S(1)}, u32[]{:S(2)}, u32[]{:S(2)}) collective-permute-start(bf16[32,3712]{1,0:T(8,128)(2,1)S(1)} %collective-permute-done.12.refs_12_), channel_id=1, source_target_pairs={{0,16},{16,128},{128,144},{144,0},{1,145},{17,1},{129,17},{145,129... | collective-permute-start | bytes 712712 | tf_op jit(solution)/shard_map/ppermute | solution.py:243
  39.0 8.1 %collective-permute-start.18 = (bf16[32,3712]{1,0:T(8,128)(2,1)S(1)}, bf16[32,3712]{1,0:T(8,128)(2,1)}, u32[]{:S(2)}, u32[]{:S(2)}) collective-permute-start(bf16[32,3712]{1,0:T(8,128)(2,1)S(1)} %collective-permute-done.14.refs_14_), channel_id=1, source_target_pairs={{1,15},{3,1},{5,3},{7,5},{9,7},{11,9},{13,11},{15,13},{17,31},{19,... | collective-permute-start | bytes 712712 | tf_op jit(solution)/shard_map/ppermute | solution.py:243
  40.9 8.8 %collective-permute-start.11 = (bf16[32,3712]{1,0:T(8,128)(2,1)S(1)}, bf16[32,3712]{1,0:T(8,128)(2,1)}, u32[]{:S(2)}, u32[]{:S(2)}) collective-permute-start(bf16[32,3712]{1,0:T(8,128)(2,1)S(1)} %collective-permute-done.10.refs_10_), channel_id=1, source_target_pairs={{0,16},{16,128},{128,144},{144,0},{1,145},{17,1},{129,17},{145,129... | collective-permute-start | bytes 712712 | tf_op jit(solution)/shard_map/ppermute | solution.py:243
  42.6 8.8 %collective-permute-start.15 = (bf16[32,3712]{1,0:T(8,128)(2,1)S(1)}, bf16[32,3712]{1,0:T(8,128)(2,1)}, u32[]{:S(2)}, u32[]{:S(2)}) collective-permute-start(bf16[32,3712]{1,0:T(8,128)(2,1)S(1)} %collective-permute-done.14.refs_14_), channel_id=1, source_target_pairs={{0,16},{16,128},{128,144},{144,0},{1,145},{17,1},{129,17},{145,129... | collective-permute-start | bytes 712712 | tf_op jit(solution)/shard_map/ppermute | solution.py:243
  43.2 8.3 %collective-permute-start.17 = (bf16[32,3712]{1,0:T(8,128)(2,1)S(1)}, bf16[32,3712]{1,0:T(8,128)(2,1)}, u32[]{:S(2)}, u32[]{:S(2)}) collective-permute-start(bf16[32,3712]{1,0:T(8,128)(2,1)S(1)} %collective-permute-done.16.refs_16_), channel_id=1, source_target_pairs={{1,145},{17,1},{129,17},{145,129},{3,147},{19,3},{131,19},{147,131... | collective-permute-start | bytes 712712 | tf_op jit(solution)/shard_map/ppermute | solution.py:243
  47.1 7.2 %collective-permute-start.19 = (bf16[32,3712]{1,0:T(8,128)(2,1)}, bf16[32,3712]{1,0:T(8,128)(2,1)}, u32[]{:S(2)}, u32[]{:S(2)}) collective-permute-start(bf16[32,3712]{1,0:T(8,128)(2,1)} %collective-permute-done.18.refs_18_), channel_id=1, source_target_pairs={{1,145},{17,1},{129,17},{145,129},{3,147},{19,3},{131,19},{147,131... | collective-permute-start | bytes 712712 | tf_op jit(solution)/shard_map/ppermute | solution.py:243
  54.2 0.9 copy-start

commit v3 on v2

--- a/solution.py
+++ b/solution.py
@@ -70,16 +70,9 @@
         copies.append(pltpu.make_async_copy(source, tiles.at[j], sems.at[j]))
         copies[j].start()
     peak[...] = jnp.full(peak.shape, -jnp.inf, jnp.float32)
-
-    def take(some):
-        for k in some:
-            place = pl.multiple_of(index_ref[HEADER + k], blocks[k].shape[0])
-            x_ref[pl.ds(place, blocks[k].shape[0]), :] = blocks[k][...]
-
-    first, last = range(4), range(len(blocks) - 4, len(blocks))
-    take(range(4, len(blocks) - 4))
-    pl.when(index_ref[2] == 0)(lambda: take(first))
-    pl.when(index_ref[2] != 0)(lambda: take(last))
+    for k, block in enumerate(blocks):
+        place = pl.multiple_of(index_ref[HEADER + k], block.shape[0])
+        x_ref[pl.ds(place, block.shape[0]), :] = block[...]
 
     for j, copy in enumerate(copies):
         copy.wait()
@@ -242,15 +235,17 @@
         axes = (axis, "c") if isinstance(axis, str) else (*axis, "c")
         return lax.ppermute(value, axes, pairs)
 
-    near = [tagged, other_half]
+    start = near = [tagged, other_half]
     blocks, where = [], []
-    for s in range(half + 1):
-        if s > 0:
-            for k in range(2):
-                near[k] = along(near[k], "z", s < half, True)
+    for s in range(1, half + 1):
+        moved = []
         for k in range(2):
-            far = along(near[k], X, s < half, s > 0)
-            blocks += [near[k], far]
+            moved.append(along(near[k], "z", s < half, True))
+        near = moved
+        for k in range(2):
+            kept = jnp.where(c == 0, start[k], near[k]) if s == half else near[k]
+            far = along(kept, X, True, True)
+            blocks += [kept, far]
             where += [(s, 0, k), (s, 1, k)]
     partner_head = hop(head, "c", 1)
 

time: 96.7 us -> 105 us (1.086)
  waiting for transfers between devices: 10.6 us -> 19.8 us
    ppermute x18 -> x16, waiting for transfers between devices: 4.52 us -> 13.8 us  [along(): return lax.ppermute(value, axes, pairs)]
    ppermute x18 -> x16, starting transfers between devices: 37 us -> 36.8 us  [along(): return lax.ppermute(value, axes, pairs)]
  transfers between devices with their start and end apart: 20 -> 18, of which waited for: 3 -> 7; matrix products, arithmetic and copies ran while one was open for 1% -> 1% of each run, Pallas kernels for 2% -> 2%
where the time goes in v3:
time: 105 us
  starting transfers between devices  40.2 us (38%)
  blocking collectives  26.1 us (25%)
  waiting for transfers between devices  19.8 us (19%)
  Pallas kernels  16.7 us (16%)
    ppermute x16, starting transfers between devices, along(): return lax.ppermute(value, axes, pairs)  36.8 us
    all_to_all x2, blocking collectives, exchange(): return lax.all_to_all(copies, axis, 0, 0, tiled=True)  26.1 us
    ppermute x16, waiting for transfers between devices, along(): return lax.ppermute(value, axes, pairs)  13.8 us
    pallas_call x1, Pallas kernels, on_device(): pl.pallas_call(score_kernel, out_shape=(jax.ShapeDtypeStruct((plane, 1, 2...  12.8 us
    ppermute x2, waiting for transfers between devices, hop(): return lax.ppermute(value, axis, [(i, (i + step) % n) for i in range(n)])  6.08 us
    ppermute x2, starting transfers between devices, hop(): return lax.ppermute(value, axis, [(i, (i + step) % n) for i in range(n)])  3.39 us
  transfers between devices with their start and end apart: 18, of which 7 were waited for; matrix products, arithmetic and copies ran while one was open for 1% of the time, Pallas kernels for 2%

profile of v3, /device:TPU:1, one launch (start us, length us, event | category | flops | bytes accessed | tf_op | source)
XLA Modules:
  0.0 104.9 jit_solution(18230692602230987680)
XLA Ops:
  0.6 3.3 %collective-permute-start = (bf16[3584,1024]{1,0:T(8,128)(2,1)}, bf16[3584,1024]{1,0:T(8,128)(2,1)}, u32[]{:S(2)}, u32[]{:S(2)}) collective-permute-start(bf16[3584,1024]{1,0:T(8,128)(2,1)} %a_ref.1), channel_id=1, source_target_pairs={{0,1},{1,0},{2,3},{3,2},{4,5},{5,4},{6,7},{7,6},{8,9},{9,8},{10,11... | collective-permute-start | bytes 22020104 | tf_op jit(solution)/shard_map/ppermute | solution.py:28
  3.9 1.7 %tag.1 = bf16[32,3712]{1,0:T(8,128)(2,1)} custom-call(bf16[32,3584]{1,0:T(8,128)(2,1)} %states_in.1, s32[1,32]{1,0:T(1,128)} %bitcast.14, f32[1,32]{1,0:T(1,128)} %bitcast.15, s32[1,32]{1,0:T(1,128)} %bitcast.16), custom_call_target="tpu_custom_call" | custom-call | tf_op jit(solution)/shard_map/tag/pallas_call | solution.py:212
  5.7 3.9 %collective-permute-start.1 = (bf16[32,3712]{1,0:T(8,128)(2,1)}, bf16[32,3712]{1,0:T(8,128)(2,1)S(1)}, u32[]{:S(2)}, u32[]{:S(2)}) collective-permute-start(bf16[32,3712]{1,0:T(8,128)(2,1)} %tag.1), channel_id=1, source_target_pairs={{0,2},{2,4},{4,6},{6,8},{8,10},{10,12},{12,14},{14,0},{1,15},{3,1}... | collective-permute-start | bytes 712712 | tf_op jit(solution)/shard_map/ppermute | solution.py:236
  9.7 6.1 %collective-permute-done.3 = bf16[32,3712]{1,0:T(8,128)(2,1)S(1)} collective-permute-done((bf16[32,3712]{1,0:T(8,128)(2,1)}, bf16[32,3712]{1,0:T(8,128)(2,1)S(1)}, u32[]{:S(2)}, u32[]{:S(2)}) %collective-permute-start.3) | collective-permute-done | bytes 237600 | tf_op jit(solution)/shard_map/ppermute | solution.py:28
  15.8 3.9 %collective-permute-start.4 = (bf16[32,3712]{1,0:T(8,128)(2,1)S(1)}, bf16[32,3712]{1,0:T(8,128)(2,1)S(1)}, u32[]{:S(2)}, u32[]{:S(2)}) collective-permute-start(bf16[32,3712]{1,0:T(8,128)(2,1)S(1)} %collective-permute-done.3), channel_id=1, source_target_pairs={{0,2},{2,4},{4,6},{6,8},{8,10},{10,12},{12,14},{14,0},{1,15},{3,1}... | collective-permute-start | bytes 712712 | tf_op jit(solution)/shard_map/ppermute | solution.py:236
  19.6 0.7 collective-permute-start.6
  20.4 2.3 %collective-permute-done.4.refs_2_ = bf16[32,3712]{1,0:T(8,128)(2,1)S(1)} collective-permute-done((bf16[32,3712]{1,0:T(8,128)(2,1)S(1)}, bf16[32,3712]{1,0:T(8,128)(2,1)S(1)}, u32[]{:S(2)}, u32[]{:S(2)}) %collective-permute-start.4) | collective-permute-done | bytes 237600 | tf_op jit(solution)/shard_map/ppermute | solution.py:236
  22.7 3.1 %collective-permute-start.8 = (bf16[32,3712]{1,0:T(8,128)(2,1)S(1)}, bf16[32,3712]{1,0:T(8,128)(2,1)S(1)}, u32[]{:S(2)}, u32[]{:S(2)}) collective-permute-start(bf16[32,3712]{1,0:T(8,128)(2,1)S(1)} %collective-permute-done.4.refs_2_), channel_id=1, source_target_pairs={{0,2},{2,4},{4,6},{6,8},{8,10},{10,12},{12,14},{14,0},{1,15},{3,1}... | collective-permute-start | bytes 712712 | tf_op jit(solution)/shard_map/ppermute | solution.py:236
  25.8 2.5 %collective-permute-start.10 = (bf16[32,3712]{1,0:T(8,128)(2,1)S(1)}, bf16[32,3712]{1,0:T(8,128)(2,1)S(1)}, u32[]{:S(2)}, u32[]{:S(2)}) collective-permute-start(bf16[32,3712]{1,0:T(8,128)(2,1)S(1)} %collective-permute-done.6.refs_4_), channel_id=1, source_target_pairs={{0,2},{2,4},{4,6},{6,8},{8,10},{10,12},{12,14},{14,0},{1,15},{3,1}... | collective-permute-start | bytes 712712 | tf_op jit(solution)/shard_map/ppermute | solution.py:236
  28.3 0.5 collective-permute-done.8.refs_6_
  28.8 3.1 %collective-permute-start.12 = (bf16[32,3712]{1,0:T(8,128)(2,1)S(1)}, bf16[32,3712]{1,0:T(8,128)(2,1)S(1)}, u32[]{:S(2)}, u32[]{:S(2)}) collective-permute-start(bf16[32,3712]{1,0:T(8,128)(2,1)S(1)} %collective-permute-done.8.refs_6_), channel_id=1, source_target_pairs={{0,2},{2,4},{4,6},{6,8},{8,10},{10,12},{12,14},{14,0},{1,15},{3,1}... | collective-permute-start | bytes 712712 | tf_op jit(solution)/shard_map/ppermute | solution.py:236
  32.0 4.4 %collective-permute-start.14 = (bf16[32,3712]{1,0:T(8,128)(2,1)S(1)}, bf16[32,3712]{1,0:T(8,128)(2,1)S(1)}, u32[]{:S(2)}, u32[]{:S(2)}) collective-permute-start(bf16[32,3712]{1,0:T(8,128)(2,1)S(1)} %collective-permute-done.10.refs_8_), channel_id=1, source_target_pairs={{1,15},{3,1},{5,3},{7,5},{9,7},{11,9},{13,11},{15,13},{17,31},{19,... | collective-permute-start | bytes 712712 | tf_op jit(solution)/shard_map/ppermute | solution.py:236
  36.4 2.6 %collective-permute-start.2 = (bf16[32,3712]{1,0:T(8,128)(2,1)S(1)}, bf16[32,3712]{1,0:T(8,128)(2,1)S(1)}, u32[]{:S(2)}, u32[]{:S(2)}) collective-permute-start(bf16[32,3712]{1,0:T(8,128)(2,1)S(1)} %collective-permute-done.1.refs_0_), channel_id=1, source_target_pairs={{0,16},{16,128},{128,144},{144,0},{1,145},{17,1},{129,17},{145,129... | collective-permute-start | bytes 712712 | tf_op jit(solution)/shard_map/ppermute | solution.py:236
  39.0 0.5 collective-permute-start.5
  39.5 0.3 collective-permute-start.7
  39.8 5.0 %collective-permute-start.16 = (bf16[32,3712]{1,0:T(8,128)(2,1)S(1)}, bf16[32,3712]{1,0:T(8,128)(2,1)S(1)}, u32[]{:S(2)}, u32[]{:S(2)}) collective-permute-start(bf16[32,3712]{1,0:T(8,128)(2,1)S(1)} %collective-permute-done.12.refs_10_), channel_id=1, source_target_pairs={{1,15},{3,1},{5,3},{7,5},{9,7},{11,9},{13,11},{15,13},{17,31},{19,... | collective-permute-start | bytes 712712 | tf_op jit(solution)/shard_map/ppermute | solution.py:236
  44.8 3.0 %collective-permute-done.16 = bf16[32,3712]{1,0:T(8,128)(2,1)S(1)} collective-permute-done((bf16[32,3712]{1,0:T(8,128)(2,1)S(1)}, bf16[32,3712]{1,0:T(8,128)(2,1)S(1)}, u32[]{:S(2)}, u32[]{:S(2)}) %collective-permute-start.16) | collective-permute-done | bytes 237600 | tf_op jit(solution)/shard_map/ppermute | solution.py:236
  47.8 2.2 %collective-permute-start.9 = (bf16[32,3712]{1,0:T(8,128)(2,1)S(1)}, bf16[32,3712]{1,0:T(8,128)(2,1)S(1)}, u32[]{:S(2)}, u32[]{:S(2)}) collective-permute-start(bf16[32,3712]{1,0:T(8,128)(2,1)S(1)} %collective-permute-done.8.refs_6_), channel_id=1, source_target_pairs={{0,16},{16,128},{128,144},{144,0},{1,145},{17,1},{129,17},{145,129... | collective-permute-start | bytes 712712 | tf_op jit(solution)/shard_map/ppermute | solution.py:236
  50.0 0.6 collective-permute-start.11
  50.7 0.3 collective-permute-start.15
  50.9 0.6 collective-permute-start.13
  51.5 1.6 %collective-permute-done.9.refs_7_ = bf16[32,3712]{1,0:T(8,128)(2,1)S(1)} collective-permute-done((bf16[32,3712]{1,0:T(8,128)(2,1)S(1)}, bf16[32,3712]{1,0:T(8,128)(2,1)S(1)}, u32[]{:S(2)}, u32[]{:S(2)}) %collective-permute-start.9) | collective-permute-done | bytes 237600 | tf_op jit(solution)/shard_map/ppermute | solution.py:236
  53.0 3.1 %collective-permute-start.17 = (bf16[32,3712]{1,0:T(8,128)(2,1)S(1)}, bf16[32,3712]{1,0:T(8,128)(2,1)}, u32[]{:S(2)}, u32[]{:S(2)}) collective-permute-start(bf16[32,3712]{1,0:T(8,128)(2,1)S(1)} %broadcast_select_fusion.refs_14_), channel_id=1, source_target_pairs={{0,16},{16,128},{128,144},{144,0},{1,145},{17,1},{129,17},{145,129... | collective-permute-start | bytes 712712 | tf_op jit(solution)/shard_map/ppermute | solution.py:236
  56.1 0.7 compare_select_fusion.7.index_ref
  56.9 3.8 %collective-permute-done.13.refs_11_ = bf16[32,3712]{1,0:T(8,128)(2,1)} collective-permute-done((bf16[32,3712]{1,0:T(8,128)(2,1)S(1)}, bf16[32,3712]{1,0:T(8,128)(2,1)}, u32[]{:S(2)}, u32[]{:S(2)}) %collective-permute-start.13) | collective-permute-done | bytes 237600 | tf_op jit(solution)/shard_map/ppermute | solution.py:236
  60.7 2.5 %collective-permute-done.17.refs_15_ = bf16[32,3712]{1,0:T(8,128)(2,1)} collective-permute-done((bf16[32,3712]{1,0:T(8,128)(2,1)S(1)}, bf16[32,3712]{1,0:T(8,128)(2,1)}, u32[]{:S(2)}, u32[]{:S(2)}) %collective-permute-start.17) | collective-permute-done | bytes 237600 | tf_op jit(solution)/shard_map/ppermute | solution.py:236
  63.2 12.8 %score.1 = (f32[16,1,1024]{2,1,0:T(1,128)S(1)}, f32[2,512]{1,0:T(2,128)S(1)}) custom-call(s32[22]{0:T(128)S(1)} %compare_select_fusion.7.index_ref, bf16[3584,1024]{1,0:T(8,128)(2,1)} %a_ref.1, bf16[3584,1024]{1,0:T(8,128)(2,1)} %collective-permute-done.b_ref, bf16[32,3712]{1,0:T(8,128)(2,1)S(1)} %collective-permute-done.1.refs_0_, ...), custom_call_target="tpu_custom_call" | custom-call | flops 7516192768 | bytes 14680064 | tf_op jit(solution)/shard_map/score/pallas_call | solution.py:264
  76.0 13.6 %all_to_all.10.parts_ref = f32[16,1,1024]{2,1,0:T(1,128)S(1)} all-to-all(f32[16,1,1024]{2,1,0:T(1,128)S(1)} %get-tuple-element.6), channel_id=1, replica_groups=mesh['xh'=2,'y'=4,'xl'=2,'z'=8,'c'=2] {'xh','xl','y'}, dimensions={0} | all-to-all | bytes 131072 | tf_op jit(solution)/shard_map/all_to_all | solution.py:32
  89.6 0.6 merge.1
  90.2 12.5 %all_to_all.11.parts_ref = f32[16,1,1152]{2,1,0:T(1,128)S(1)} all-to-all(f32[16,1,1152]{2,1,0:T(1,128)S(1)} %merge.1), channel_id=1, replica_groups=mesh['xh'=2,'y'=4,'xl'=2,'z'=8,'c'=2] {'z','c'}, dimensions={0} | all-to-all | bytes 147456 | tf_op jit(solution)/shard_map/all_to_all | solution.py:32
  102.8 1.6 %finish.1 = (f32[1,128]{1,0:T(1,128)S(1)}, f32[1,512]{1,0:T(1,128)}) custom-call(s32[22]{0:T(128)S(1)} %compare_select_fusion.7.index_ref, f32[16,1,1152]{2,1,0:T(1,128)S(1)} %all_to_all.11.parts_ref), custom_call_target="tpu_custom_call" | custom-call | tf_op jit(solution)/shard_map/finish/pallas_call | solution.py:293
  104.4 0.5 slice_bitcast_fusion
  (14 shorter events, 0.2 us)
Async XLA Ops:
  0.6 62.6 %collective-permute-start = (bf16[3584,1024]{1,0:T(8,128)(2,1)}, bf16[3584,1024]{1,0:T(8,128)(2,1)}, u32[]{:S(2)}, u32[]{:S(2)}) collective-permute-start(bf16[3584,1024]{1,0:T(8,128)(2,1)} %a_ref.1), channel_id=1, source_target_pairs={{0,1},{1,0},{2,3},{3,2},{4,5},{5,4},{6,7},{7,6},{8,9},{9,8},{10,11... | collective-permute-start | bytes 22020104 | tf_op jit(solution)/shard_map/ppermute | solution.py:28
  5.6 10.1 %collective-permute-start.3 = (bf16[32,3712]{1,0:T(8,128)(2,1)}, bf16[32,3712]{1,0:T(8,128)(2,1)S(1)}, u32[]{:S(2)}, u32[]{:S(2)}) collective-permute-start(bf16[32,3712]{1,0:T(8,128)(2,1)} %tag.1), channel_id=1, source_target_pairs={{0,1},{1,0},{2,3},{3,2},{4,5},{5,4},{6,7},{7,6},{8,9},{9,8},{10,11... | collective-permute-start | bytes 712712 | tf_op jit(solution)/shard_map/ppermute | solution.py:28
  5.7 13.9 %collective-permute-start.1 = (bf16[32,3712]{1,0:T(8,128)(2,1)}, bf16[32,3712]{1,0:T(8,128)(2,1)S(1)}, u32[]{:S(2)}, u32[]{:S(2)}) collective-permute-start(bf16[32,3712]{1,0:T(8,128)(2,1)} %tag.1), channel_id=1, source_target_pairs={{0,2},{2,4},{4,6},{6,8},{8,10},{10,12},{12,14},{14,0},{1,15},{3,1}... | collective-permute-start | bytes 712712 | tf_op jit(solution)/shard_map/ppermute | solution.py:236
  15.8 6.9 %collective-permute-start.4 = (bf16[32,3712]{1,0:T(8,128)(2,1)S(1)}, bf16[32,3712]{1,0:T(8,128)(2,1)S(1)}, u32[]{:S(2)}, u32[]{:S(2)}) collective-permute-start(bf16[32,3712]{1,0:T(8,128)(2,1)S(1)} %collective-permute-done.3), channel_id=1, source_target_pairs={{0,2},{2,4},{4,6},{6,8},{8,10},{10,12},{12,14},{14,0},{1,15},{3,1}... | collective-permute-start | bytes 712712 | tf_op jit(solution)/shard_map/ppermute | solution.py:236
  19.6 6.2 %collective-permute-start.6 = (bf16[32,3712]{1,0:T(8,128)(2,1)S(1)}, bf16[32,3712]{1,0:T(8,128)(2,1)S(1)}, u32[]{:S(2)}, u32[]{:S(2)}) collective-permute-start(bf16[32,3712]{1,0:T(8,128)(2,1)S(1)} %collective-permute-done.1.refs_0_), channel_id=1, source_target_pairs={{0,2},{2,4},{4,6},{6,8},{8,10},{10,12},{12,14},{14,0},{1,15},{3,1}... | collective-permute-start | bytes 712712 | tf_op jit(solution)/shard_map/ppermute | solution.py:236
  22.7 6.2 %collective-permute-start.8 = (bf16[32,3712]{1,0:T(8,128)(2,1)S(1)}, bf16[32,3712]{1,0:T(8,128)(2,1)S(1)}, u32[]{:S(2)}, u32[]{:S(2)}) collective-permute-start(bf16[32,3712]{1,0:T(8,128)(2,1)S(1)} %collective-permute-done.4.refs_2_), channel_id=1, source_target_pairs={{0,2},{2,4},{4,6},{6,8},{8,10},{10,12},{12,14},{14,0},{1,15},{3,1}... | collective-permute-start | bytes 712712 | tf_op jit(solution)/shard_map/ppermute | solution.py:236
  25.8 6.2 %collective-permute-start.10 = (bf16[32,3712]{1,0:T(8,128)(2,1)S(1)}, bf16[32,3712]{1,0:T(8,128)(2,1)S(1)}, u32[]{:S(2)}, u32[]{:S(2)}) collective-permute-start(bf16[32,3712]{1,0:T(8,128)(2,1)S(1)} %collective-permute-done.6.refs_4_), channel_id=1, source_target_pairs={{0,2},{2,4},{4,6},{6,8},{8,10},{10,12},{12,14},{14,0},{1,15},{3,1}... | collective-permute-start | bytes 712712 | tf_op jit(solution)/shard_map/ppermute | solution.py:236
  28.8 10.7 %collective-permute-start.12 = (bf16[32,3712]{1,0:T(8,128)(2,1)S(1)}, bf16[32,3712]{1,0:T(8,128)(2,1)S(1)}, u32[]{:S(2)}, u32[]{:S(2)}) collective-permute-start(bf16[32,3712]{1,0:T(8,128)(2,1)S(1)} %collective-permute-done.8.refs_6_), channel_id=1, source_target_pairs={{0,2},{2,4},{4,6},{6,8},{8,10},{10,12},{12,14},{14,0},{1,15},{3,1}... | collective-permute-start | bytes 712712 | tf_op jit(solution)/shard_map/ppermute | solution.py:236
  32.0 7.8 %collective-permute-start.14 = (bf16[32,3712]{1,0:T(8,128)(2,1)S(1)}, bf16[32,3712]{1,0:T(8,128)(2,1)S(1)}, u32[]{:S(2)}, u32[]{:S(2)}) collective-permute-start(bf16[32,3712]{1,0:T(8,128)(2,1)S(1)} %collective-permute-done.10.refs_8_), channel_id=1, source_target_pairs={{1,15},{3,1},{5,3},{7,5},{9,7},{11,9},{13,11},{15,13},{17,31},{19,... | collective-permute-start | bytes 712712 | tf_op jit(solution)/shard_map/ppermute | solution.py:236
  36.4 13.6 %collective-permute-start.2 = (bf16[32,3712]{1,0:T(8,128)(2,1)S(1)}, bf16[32,3712]{1,0:T(8,128)(2,1)S(1)}, u32[]{:S(2)}, u32[]{:S(2)}) collective-permute-start(bf16[32,3712]{1,0:T(8,128)(2,1)S(1)} %collective-permute-done.1.refs_0_), channel_id=1, source_target_pairs={{0,16},{16,128},{128,144},{144,0},{1,145},{17,1},{129,17},{145,129... | collective-permute-start | bytes 712712 | tf_op jit(solution)/shard_map/ppermute | solution.py:236
  39.0 11.7 %collective-permute-start.5 = (bf16[32,3712]{1,0:T(8,128)(2,1)S(1)}, bf16[32,3712]{1,0:T(8,128)(2,1)S(1)}, u32[]{:S(2)}, u32[]{:S(2)}) collective-permute-start(bf16[32,3712]{1,0:T(8,128)(2,1)S(1)} %collective-permute-done.4.refs_2_), channel_id=1, source_target_pairs={{0,16},{16,128},{128,144},{144,0},{1,145},{17,1},{129,17},{145,129... | collective-permute-start | bytes 712712 | tf_op jit(solution)/shard_map/ppermute | solution.py:236
  39.5 11.4 %collective-permute-start.7 = (bf16[32,3712]{1,0:T(8,128)(2,1)S(1)}, bf16[32,3712]{1,0:T(8,128)(2,1)S(1)}, u32[]{:S(2)}, u32[]{:S(2)}) collective-permute-start(bf16[32,3712]{1,0:T(8,128)(2,1)S(1)} %collective-permute-done.6.refs_4_), channel_id=1, source_target_pairs={{0,16},{16,128},{128,144},{144,0},{1,145},{17,1},{129,17},{145,129... | collective-permute-start | bytes 712712 | tf_op jit(solution)/shard_map/ppermute | solution.py:236
  39.8 8.0 %collective-permute-start.16 = (bf16[32,3712]{1,0:T(8,128)(2,1)S(1)}, bf16[32,3712]{1,0:T(8,128)(2,1)S(1)}, u32[]{:S(2)}, u32[]{:S(2)}) collective-permute-start(bf16[32,3712]{1,0:T(8,128)(2,1)S(1)} %collective-permute-done.12.refs_10_), channel_id=1, source_target_pairs={{1,15},{3,1},{5,3},{7,5},{9,7},{11,9},{13,11},{15,13},{17,31},{19,... | collective-permute-start | bytes 712712 | tf_op jit(solution)/shard_map/ppermute | solution.py:236
  47.8 5.3 %collective-permute-start.9 = (bf16[32,3712]{1,0:T(8,128)(2,1)S(1)}, bf16[32,3712]{1,0:T(8,128)(2,1)S(1)}, u32[]{:S(2)}, u32[]{:S(2)}) collective-permute-start(bf16[32,3712]{1,0:T(8,128)(2,1)S(1)} %collective-permute-done.8.refs_6_), channel_id=1, source_target_pairs={{0,16},{16,128},{128,144},{144,0},{1,145},{17,1},{129,17},{145,129... | collective-permute-start | bytes 712712 | tf_op jit(solution)/shard_map/ppermute | solution.py:236
  50.0 6.8 %collective-permute-start.11 = (bf16[32,3712]{1,0:T(8,128)(2,1)S(1)}, bf16[32,3712]{1,0:T(8,128)(2,1)S(1)}, u32[]{:S(2)}, u32[]{:S(2)}) collective-permute-start(bf16[32,3712]{1,0:T(8,128)(2,1)S(1)} %collective-permute-done.10.refs_8_), channel_id=1, source_target_pairs={{0,16},{16,128},{128,144},{144,0},{1,145},{17,1},{129,17},{145,129... | collective-permute-start | bytes 712712 | tf_op jit(solution)/shard_map/ppermute | solution.py:236
  50.7 10.0 %collective-permute-start.15 = (bf16[32,3712]{1,0:T(8,128)(2,1)S(1)}, bf16[32,3712]{1,0:T(8,128)(2,1)S(1)}, u32[]{:S(2)}, u32[]{:S(2)}) collective-permute-start(bf16[32,3712]{1,0:T(8,128)(2,1)S(1)} %broadcast_select_fusion.1.refs_12_), channel_id=1, source_target_pairs={{0,16},{16,128},{128,144},{144,0},{1,145},{17,1},{129,17},{145,129... | collective-permute-start | bytes 712712 | tf_op jit(solution)/shard_map/ppermute | solution.py:236
  50.9 9.7 %collective-permute-start.13 = (bf16[32,3712]{1,0:T(8,128)(2,1)S(1)}, bf16[32,3712]{1,0:T(8,128)(2,1)}, u32[]{:S(2)}, u32[]{:S(2)}) collective-permute-start(bf16[32,3712]{1,0:T(8,128)(2,1)S(1)} %collective-permute-done.12.refs_10_), channel_id=1, source_target_pairs={{0,16},{16,128},{128,144},{144,0},{1,145},{17,1},{129,17},{145,129... | collective-permute-start | bytes 712712 | tf_op jit(solution)/shard_map/ppermute | solution.py:236
  53.0 10.2 %collective-permute-start.17 = (bf16[32,3712]{1,0:T(8,128)(2,1)S(1)}, bf16[32,3712]{1,0:T(8,128)(2,1)}, u32[]{:S(2)}, u32[]{:S(2)}) collective-permute-start(bf16[32,3712]{1,0:T(8,128)(2,1)S(1)} %broadcast_select_fusion.refs_14_), channel_id=1, source_target_pairs={{0,16},{16,128},{128,144},{144,0},{1,145},{17,1},{129,17},{145,129... | collective-permute-start | bytes 712712 | tf_op jit(solution)/shard_map/ppermute | solution.py:236

commit v4 on v3

--- a/solution.py
+++ b/solution.py
@@ -200,7 +200,7 @@
         sums = part if sums is None else sums + part
     score_ref[...] = (sums[0:1] + sums[1:2] + sums[2:3]) / sums[3:4]
     mine = jnp.where(index_ref[4] == 0, excesses[0], excesses[1])
-    own_ref[...] = pltpu.roll(mine, lax.rem(rows - index_ref[3], rows), 1)[:, :LANES]
+    own_ref[...] = pltpu.roll(mine, lax.rem(rows - index_ref[3], rows), 1)[:, : own_ref.shape[1]]
 
 
 def on_device(states, head, targets, ref_loss, seq_ids):
@@ -293,7 +293,7 @@
     own, score = pl.pallas_call(
         functools.partial(finish_kernel, nz=nz, span=span),
         out_shape=(
-            jax.ShapeDtypeStruct((1, LANES), jnp.float32),
+            jax.ShapeDtypeStruct((1, local), jnp.float32),
             jax.ShapeDtypeStruct((1, tokens), jnp.float32),
         ),
         in_specs=[SMEM, VMEM],
@@ -301,7 +301,7 @@
         compiler_params=pltpu.CompilerParams(vmem_limit_bytes=8 << 20),
         name="finish",
     )(index, exchange(stats, ("z", "c")))
-    return own[0, :local], score[0]
+    return own[0], score[0]
 
 
 def solution(mesh):

time: 105 us -> 105 us (level)
  no operation moved by 1% of the time
where the time goes in v4:
time: 105 us; the launch traced here: 104 us
  starting transfers between devices  40.2 us (38%)
  blocking collectives  26.1 us (25%)
  waiting for transfers between devices  19.8 us (19%)
  Pallas kernels  16.7 us (16%)
    ppermute x16, starting transfers between devices, along(): return lax.ppermute(value, axes, pairs)  36.8 us
    all_to_all x2, blocking collectives, exchange(): return lax.all_to_all(copies, axis, 0, 0, tiled=True)  26.1 us
    ppermute x16, waiting for transfers between devices, along(): return lax.ppermute(value, axes, pairs)  13.8 us
    pallas_call x1, Pallas kernels, on_device(): pl.pallas_call(score_kernel, out_shape=(jax.ShapeDtypeStruct((plane, 1, 2...  12.8 us
    ppermute x2, waiting for transfers between devices, hop(): return lax.ppermute(value, axis, [(i, (i + step) % n) for i in range(n)])  6.08 us
    ppermute x2, starting transfers between devices, hop(): return lax.ppermute(value, axis, [(i, (i + step) % n) for i in range(n)])  3.39 us
  transfers between devices with their start and end apart: 18, of which 7 were waited for; matrix products, arithmetic and copies ran while one was open for 1% of the time, Pallas kernels for 2%

profile of v4, /device:TPU:1, one launch (start us, length us, event | category | flops | bytes accessed | tf_op | source)
XLA Modules:
  0.0 104.4 jit_solution(9405864695903966432)
XLA Ops:
  0.6 3.3 %collective-permute-start = (bf16[3584,1024]{1,0:T(8,128)(2,1)}, bf16[3584,1024]{1,0:T(8,128)(2,1)}, u32[]{:S(2)}, u32[]{:S(2)}) collective-permute-start(bf16[3584,1024]{1,0:T(8,128)(2,1)} %a_ref.1), channel_id=1, source_target_pairs={{0,1},{1,0},{2,3},{3,2},{4,5},{5,4},{6,7},{7,6},{8,9},{9,8},{10,11... | collective-permute-start | bytes 22020104 | tf_op jit(solution)/shard_map/ppermute | solution.py:28
  3.9 1.7 %tag.1 = bf16[32,3712]{1,0:T(8,128)(2,1)} custom-call(bf16[32,3584]{1,0:T(8,128)(2,1)} %states_in.1, s32[1,32]{1,0:T(1,128)} %bitcast.13, f32[1,32]{1,0:T(1,128)} %bitcast.14, s32[1,32]{1,0:T(1,128)} %bitcast.15), custom_call_target="tpu_custom_call" | custom-call | tf_op jit(solution)/shard_map/tag/pallas_call | solution.py:212
  5.6 0.1 collective-permute-start.3
  5.7 3.9 %collective-permute-start.1 = (bf16[32,3712]{1,0:T(8,128)(2,1)}, bf16[32,3712]{1,0:T(8,128)(2,1)S(1)}, u32[]{:S(2)}, u32[]{:S(2)}) collective-permute-start(bf16[32,3712]{1,0:T(8,128)(2,1)} %tag.1), channel_id=1, source_target_pairs={{0,2},{2,4},{4,6},{6,8},{8,10},{10,12},{12,14},{14,0},{1,15},{3,1}... | collective-permute-start | bytes 712712 | tf_op jit(solution)/shard_map/ppermute | solution.py:236
  9.7 6.1 %collective-permute-done.3 = bf16[32,3712]{1,0:T(8,128)(2,1)S(1)} collective-permute-done((bf16[32,3712]{1,0:T(8,128)(2,1)}, bf16[32,3712]{1,0:T(8,128)(2,1)S(1)}, u32[]{:S(2)}, u32[]{:S(2)}) %collective-permute-start.3) | collective-permute-done | bytes 237600 | tf_op jit(solution)/shard_map/ppermute | solution.py:28
  15.8 3.9 %collective-permute-start.4 = (bf16[32,3712]{1,0:T(8,128)(2,1)S(1)}, bf16[32,3712]{1,0:T(8,128)(2,1)S(1)}, u32[]{:S(2)}, u32[]{:S(2)}) collective-permute-start(bf16[32,3712]{1,0:T(8,128)(2,1)S(1)} %collective-permute-done.3), channel_id=1, source_target_pairs={{0,2},{2,4},{4,6},{6,8},{8,10},{10,12},{12,14},{14,0},{1,15},{3,1}... | collective-permute-start | bytes 712712 | tf_op jit(solution)/shard_map/ppermute | solution.py:236
  19.6 0.7 collective-permute-start.6
  20.4 2.3 %collective-permute-done.4.refs_2_ = bf16[32,3712]{1,0:T(8,128)(2,1)S(1)} collective-permute-done((bf16[32,3712]{1,0:T(8,128)(2,1)S(1)}, bf16[32,3712]{1,0:T(8,128)(2,1)S(1)}, u32[]{:S(2)}, u32[]{:S(2)}) %collective-permute-start.4) | collective-permute-done | bytes 237600 | tf_op jit(solution)/shard_map/ppermute | solution.py:236
  22.7 3.1 %collective-permute-start.8 = (bf16[32,3712]{1,0:T(8,128)(2,1)S(1)}, bf16[32,3712]{1,0:T(8,128)(2,1)S(1)}, u32[]{:S(2)}, u32[]{:S(2)}) collective-permute-start(bf16[32,3712]{1,0:T(8,128)(2,1)S(1)} %collective-permute-done.4.refs_2_), channel_id=1, source_target_pairs={{0,2},{2,4},{4,6},{6,8},{8,10},{10,12},{12,14},{14,0},{1,15},{3,1}... | collective-permute-start | bytes 712712 | tf_op jit(solution)/shard_map/ppermute | solution.py:236
  25.8 2.5 %collective-permute-start.10 = (bf16[32,3712]{1,0:T(8,128)(2,1)S(1)}, bf16[32,3712]{1,0:T(8,128)(2,1)S(1)}, u32[]{:S(2)}, u32[]{:S(2)}) collective-permute-start(bf16[32,3712]{1,0:T(8,128)(2,1)S(1)} %collective-permute-done.6.refs_4_), channel_id=1, source_target_pairs={{0,2},{2,4},{4,6},{6,8},{8,10},{10,12},{12,14},{14,0},{1,15},{3,1}... | collective-permute-start | bytes 712712 | tf_op jit(solution)/shard_map/ppermute | solution.py:236
  28.3 0.5 collective-permute-done.8.refs_6_
  28.8 3.1 %collective-permute-start.12 = (bf16[32,3712]{1,0:T(8,128)(2,1)S(1)}, bf16[32,3712]{1,0:T(8,128)(2,1)S(1)}, u32[]{:S(2)}, u32[]{:S(2)}) collective-permute-start(bf16[32,3712]{1,0:T(8,128)(2,1)S(1)} %collective-permute-done.8.refs_6_), channel_id=1, source_target_pairs={{0,2},{2,4},{4,6},{6,8},{8,10},{10,12},{12,14},{14,0},{1,15},{3,1}... | collective-permute-start | bytes 712712 | tf_op jit(solution)/shard_map/ppermute | solution.py:236
  32.0 4.4 %collective-permute-start.14 = (bf16[32,3712]{1,0:T(8,128)(2,1)S(1)}, bf16[32,3712]{1,0:T(8,128)(2,1)S(1)}, u32[]{:S(2)}, u32[]{:S(2)}) collective-permute-start(bf16[32,3712]{1,0:T(8,128)(2,1)S(1)} %collective-permute-done.10.refs_8_), channel_id=1, source_target_pairs={{1,15},{3,1},{5,3},{7,5},{9,7},{11,9},{13,11},{15,13},{17,31},{19,... | collective-permute-start | bytes 712712 | tf_op jit(solution)/shard_map/ppermute | solution.py:236
  36.4 2.6 %collective-permute-start.2 = (bf16[32,3712]{1,0:T(8,128)(2,1)S(1)}, bf16[32,3712]{1,0:T(8,128)(2,1)S(1)}, u32[]{:S(2)}, u32[]{:S(2)}) collective-permute-start(bf16[32,3712]{1,0:T(8,128)(2,1)S(1)} %collective-permute-done.1.refs_0_), channel_id=1, source_target_pairs={{0,16},{16,128},{128,144},{144,0},{1,145},{17,1},{129,17},{145,129... | collective-permute-start | bytes 712712 | tf_op jit(solution)/shard_map/ppermute | solution.py:236
  39.0 0.5 collective-permute-start.5
  39.5 0.3 collective-permute-start.7
  39.8 5.0 %collective-permute-start.16 = (bf16[32,3712]{1,0:T(8,128)(2,1)S(1)}, bf16[32,3712]{1,0:T(8,128)(2,1)S(1)}, u32[]{:S(2)}, u32[]{:S(2)}) collective-permute-start(bf16[32,3712]{1,0:T(8,128)(2,1)S(1)} %collective-permute-done.12.refs_10_), channel_id=1, source_target_pairs={{1,15},{3,1},{5,3},{7,5},{9,7},{11,9},{13,11},{15,13},{17,31},{19,... | collective-permute-start | bytes 712712 | tf_op jit(solution)/shard_map/ppermute | solution.py:236
  44.8 3.0 %collective-permute-done.16 = bf16[32,3712]{1,0:T(8,128)(2,1)S(1)} collective-permute-done((bf16[32,3712]{1,0:T(8,128)(2,1)S(1)}, bf16[32,3712]{1,0:T(8,128)(2,1)S(1)}, u32[]{:S(2)}, u32[]{:S(2)}) %collective-permute-start.16) | collective-permute-done | bytes 237600 | tf_op jit(solution)/shard_map/ppermute | solution.py:236
  47.8 2.2 %collective-permute-start.9 = (bf16[32,3712]{1,0:T(8,128)(2,1)S(1)}, bf16[32,3712]{1,0:T(8,128)(2,1)S(1)}, u32[]{:S(2)}, u32[]{:S(2)}) collective-permute-start(bf16[32,3712]{1,0:T(8,128)(2,1)S(1)} %collective-permute-done.8.refs_6_), channel_id=1, source_target_pairs={{0,16},{16,128},{128,144},{144,0},{1,145},{17,1},{129,17},{145,129... | collective-permute-start | bytes 712712 | tf_op jit(solution)/shard_map/ppermute | solution.py:236
  50.0 0.6 collective-permute-start.11
  50.7 0.3 collective-permute-start.15
  50.9 0.6 collective-permute-start.13
  51.5 1.6 %collective-permute-done.9.refs_7_ = bf16[32,3712]{1,0:T(8,128)(2,1)S(1)} collective-permute-done((bf16[32,3712]{1,0:T(8,128)(2,1)S(1)}, bf16[32,3712]{1,0:T(8,128)(2,1)S(1)}, u32[]{:S(2)}, u32[]{:S(2)}) %collective-permute-start.9) | collective-permute-done | bytes 237600 | tf_op jit(solution)/shard_map/ppermute | solution.py:236
  53.0 3.1 %collective-permute-start.17 = (bf16[32,3712]{1,0:T(8,128)(2,1)S(1)}, bf16[32,3712]{1,0:T(8,128)(2,1)}, u32[]{:S(2)}, u32[]{:S(2)}) collective-permute-start(bf16[32,3712]{1,0:T(8,128)(2,1)S(1)} %broadcast_select_fusion.refs_14_), channel_id=1, source_target_pairs={{0,16},{16,128},{128,144},{144,0},{1,145},{17,1},{129,17},{145,129... | collective-permute-start | bytes 712712 | tf_op jit(solution)/shard_map/ppermute | solution.py:236
  56.1 0.7 compare_select_fusion.7.index_ref
  56.9 3.8 %collective-permute-done.13.refs_11_ = bf16[32,3712]{1,0:T(8,128)(2,1)} collective-permute-done((bf16[32,3712]{1,0:T(8,128)(2,1)S(1)}, bf16[32,3712]{1,0:T(8,128)(2,1)}, u32[]{:S(2)}, u32[]{:S(2)}) %collective-permute-start.13) | collective-permute-done | bytes 237600 | tf_op jit(solution)/shard_map/ppermute | solution.py:236
  60.7 2.5 %collective-permute-done.17.refs_15_ = bf16[32,3712]{1,0:T(8,128)(2,1)} collective-permute-done((bf16[32,3712]{1,0:T(8,128)(2,1)S(1)}, bf16[32,3712]{1,0:T(8,128)(2,1)}, u32[]{:S(2)}, u32[]{:S(2)}) %collective-permute-start.17) | collective-permute-done | bytes 237600 | tf_op jit(solution)/shard_map/ppermute | solution.py:236
  63.2 12.8 %score.1 = (f32[16,1,1024]{2,1,0:T(1,128)S(1)}, f32[2,512]{1,0:T(2,128)S(1)}) custom-call(s32[22]{0:T(128)S(1)} %compare_select_fusion.7.index_ref, bf16[3584,1024]{1,0:T(8,128)(2,1)} %a_ref.1, bf16[3584,1024]{1,0:T(8,128)(2,1)} %collective-permute-done.b_ref, bf16[32,3712]{1,0:T(8,128)(2,1)S(1)} %collective-permute-done.1.refs_0_, ...), custom_call_target="tpu_custom_call" | custom-call | flops 7516192768 | bytes 14680064 | tf_op jit(solution)/shard_map/score/pallas_call | solution.py:264
  76.0 13.6 %all_to_all.10.parts_ref = f32[16,1,1024]{2,1,0:T(1,128)S(1)} all-to-all(f32[16,1,1024]{2,1,0:T(1,128)S(1)} %get-tuple-element.6), channel_id=1, replica_groups=mesh['xh'=2,'y'=4,'xl'=2,'z'=8,'c'=2] {'xh','xl','y'}, dimensions={0} | all-to-all | bytes 131072 | tf_op jit(solution)/shard_map/all_to_all | solution.py:32
  89.6 0.6 merge.1
  90.2 12.5 %all_to_all.11.parts_ref = f32[16,1,1152]{2,1,0:T(1,128)S(1)} all-to-all(f32[16,1,1152]{2,1,0:T(1,128)S(1)} %merge.1), channel_id=1, replica_groups=mesh['xh'=2,'y'=4,'xl'=2,'z'=8,'c'=2] {'z','c'}, dimensions={0} | all-to-all | bytes 147456 | tf_op jit(solution)/shard_map/all_to_all | solution.py:32
  102.8 1.6 %finish.1 = (f32[1,32]{1,0:T(1,128)}, f32[1,512]{1,0:T(1,128)}) custom-call(s32[22]{0:T(128)S(1)} %compare_select_fusion.7.index_ref, f32[16,1,1152]{2,1,0:T(1,128)S(1)} %all_to_all.11.parts_ref), custom_call_target="tpu_custom_call" | custom-call | tf_op jit(solution)/shard_map/finish/pallas_call | solution.py:293
  (13 shorter events, 0.1 us)
Async XLA Ops:
  0.6 62.6 %collective-permute-start = (bf16[3584,1024]{1,0:T(8,128)(2,1)}, bf16[3584,1024]{1,0:T(8,128)(2,1)}, u32[]{:S(2)}, u32[]{:S(2)}) collective-permute-start(bf16[3584,1024]{1,0:T(8,128)(2,1)} %a_ref.1), channel_id=1, source_target_pairs={{0,1},{1,0},{2,3},{3,2},{4,5},{5,4},{6,7},{7,6},{8,9},{9,8},{10,11... | collective-permute-start | bytes 22020104 | tf_op jit(solution)/shard_map/ppermute | solution.py:28
  5.6 10.1 %collective-permute-start.3 = (bf16[32,3712]{1,0:T(8,128)(2,1)}, bf16[32,3712]{1,0:T(8,128)(2,1)S(1)}, u32[]{:S(2)}, u32[]{:S(2)}) collective-permute-start(bf16[32,3712]{1,0:T(8,128)(2,1)} %tag.1), channel_id=1, source_target_pairs={{0,1},{1,0},{2,3},{3,2},{4,5},{5,4},{6,7},{7,6},{8,9},{9,8},{10,11... | collective-permute-start | bytes 712712 | tf_op jit(solution)/shard_map/ppermute | solution.py:28
  5.7 13.9 %collective-permute-start.1 = (bf16[32,3712]{1,0:T(8,128)(2,1)}, bf16[32,3712]{1,0:T(8,128)(2,1)S(1)}, u32[]{:S(2)}, u32[]{:S(2)}) collective-permute-start(bf16[32,3712]{1,0:T(8,128)(2,1)} %tag.1), channel_id=1, source_target_pairs={{0,2},{2,4},{4,6},{6,8},{8,10},{10,12},{12,14},{14,0},{1,15},{3,1}... | collective-permute-start | bytes 712712 | tf_op jit(solution)/shard_map/ppermute | solution.py:236
  15.8 6.9 %collective-permute-start.4 = (bf16[32,3712]{1,0:T(8,128)(2,1)S(1)}, bf16[32,3712]{1,0:T(8,128)(2,1)S(1)}, u32[]{:S(2)}, u32[]{:S(2)}) collective-permute-start(bf16[32,3712]{1,0:T(8,128)(2,1)S(1)} %collective-permute-done.3), channel_id=1, source_target_pairs={{0,2},{2,4},{4,6},{6,8},{8,10},{10,12},{12,14},{14,0},{1,15},{3,1}... | collective-permute-start | bytes 712712 | tf_op jit(solution)/shard_map/ppermute | solution.py:236
  19.6 6.2 %collective-permute-start.6 = (bf16[32,3712]{1,0:T(8,128)(2,1)S(1)}, bf16[32,3712]{1,0:T(8,128)(2,1)S(1)}, u32[]{:S(2)}, u32[]{:S(2)}) collective-permute-start(bf16[32,3712]{1,0:T(8,128)(2,1)S(1)} %collective-permute-done.1.refs_0_), channel_id=1, source_target_pairs={{0,2},{2,4},{4,6},{6,8},{8,10},{10,12},{12,14},{14,0},{1,15},{3,1}... | collective-permute-start | bytes 712712 | tf_op jit(solution)/shard_map/ppermute | solution.py:236
  22.7 6.2 %collective-permute-start.8 = (bf16[32,3712]{1,0:T(8,128)(2,1)S(1)}, bf16[32,3712]{1,0:T(8,128)(2,1)S(1)}, u32[]{:S(2)}, u32[]{:S(2)}) collective-permute-start(bf16[32,3712]{1,0:T(8,128)(2,1)S(1)} %collective-permute-done.4.refs_2_), channel_id=1, source_target_pairs={{0,2},{2,4},{4,6},{6,8},{8,10},{10,12},{12,14},{14,0},{1,15},{3,1}... | collective-permute-start | bytes 712712 | tf_op jit(solution)/shard_map/ppermute | solution.py:236
  25.8 6.2 %collective-permute-start.10 = (bf16[32,3712]{1,0:T(8,128)(2,1)S(1)}, bf16[32,3712]{1,0:T(8,128)(2,1)S(1)}, u32[]{:S(2)}, u32[]{:S(2)}) collective-permute-start(bf16[32,3712]{1,0:T(8,128)(2,1)S(1)} %collective-permute-done.6.refs_4_), channel_id=1, source_target_pairs={{0,2},{2,4},{4,6},{6,8},{8,10},{10,12},{12,14},{14,0},{1,15},{3,1}... | collective-permute-start | bytes 712712 | tf_op jit(solution)/shard_map/ppermute | solution.py:236
  28.8 10.7 %collective-permute-start.12 = (bf16[32,3712]{1,0:T(8,128)(2,1)S(1)}, bf16[32,3712]{1,0:T(8,128)(2,1)S(1)}, u32[]{:S(2)}, u32[]{:S(2)}) collective-permute-start(bf16[32,3712]{1,0:T(8,128)(2,1)S(1)} %collective-permute-done.8.refs_6_), channel_id=1, source_target_pairs={{0,2},{2,4},{4,6},{6,8},{8,10},{10,12},{12,14},{14,0},{1,15},{3,1}... | collective-permute-start | bytes 712712 | tf_op jit(solution)/shard_map/ppermute | solution.py:236
  32.0 7.8 %collective-permute-start.14 = (bf16[32,3712]{1,0:T(8,128)(2,1)S(1)}, bf16[32,3712]{1,0:T(8,128)(2,1)S(1)}, u32[]{:S(2)}, u32[]{:S(2)}) collective-permute-start(bf16[32,3712]{1,0:T(8,128)(2,1)S(1)} %collective-permute-done.10.refs_8_), channel_id=1, source_target_pairs={{1,15},{3,1},{5,3},{7,5},{9,7},{11,9},{13,11},{15,13},{17,31},{19,... | collective-permute-start | bytes 712712 | tf_op jit(solution)/shard_map/ppermute | solution.py:236
  36.4 13.6 %collective-permute-start.2 = (bf16[32,3712]{1,0:T(8,128)(2,1)S(1)}, bf16[32,3712]{1,0:T(8,128)(2,1)S(1)}, u32[]{:S(2)}, u32[]{:S(2)}) collective-permute-start(bf16[32,3712]{1,0:T(8,128)(2,1)S(1)} %collective-permute-done.1.refs_0_), channel_id=1, source_target_pairs={{0,16},{16,128},{128,144},{144,0},{1,145},{17,1},{129,17},{145,129... | collective-permute-start | bytes 712712 | tf_op jit(solution)/shard_map/ppermute | solution.py:236
  39.0 11.7 %collective-permute-start.5 = (bf16[32,3712]{1,0:T(8,128)(2,1)S(1)}, bf16[32,3712]{1,0:T(8,128)(2,1)S(1)}, u32[]{:S(2)}, u32[]{:S(2)}) collective-permute-start(bf16[32,3712]{1,0:T(8,128)(2,1)S(1)} %collective-permute-done.4.refs_2_), channel_id=1, source_target_pairs={{0,16},{16,128},{128,144},{144,0},{1,145},{17,1},{129,17},{145,129... | collective-permute-start | bytes 712712 | tf_op jit(solution)/shard_map/ppermute | solution.py:236
  39.5 11.4 %collective-permute-start.7 = (bf16[32,3712]{1,0:T(8,128)(2,1)S(1)}, bf16[32,3712]{1,0:T(8,128)(2,1)S(1)}, u32[]{:S(2)}, u32[]{:S(2)}) collective-permute-start(bf16[32,3712]{1,0:T(8,128)(2,1)S(1)} %collective-permute-done.6.refs_4_), channel_id=1, source_target_pairs={{0,16},{16,128},{128,144},{144,0},{1,145},{17,1},{129,17},{145,129... | collective-permute-start | bytes 712712 | tf_op jit(solution)/shard_map/ppermute | solution.py:236
  39.8 8.0 %collective-permute-start.16 = (bf16[32,3712]{1,0:T(8,128)(2,1)S(1)}, bf16[32,3712]{1,0:T(8,128)(2,1)S(1)}, u32[]{:S(2)}, u32[]{:S(2)}) collective-permute-start(bf16[32,3712]{1,0:T(8,128)(2,1)S(1)} %collective-permute-done.12.refs_10_), channel_id=1, source_target_pairs={{1,15},{3,1},{5,3},{7,5},{9,7},{11,9},{13,11},{15,13},{17,31},{19,... | collective-permute-start | bytes 712712 | tf_op jit(solution)/shard_map/ppermute | solution.py:236
  47.8 5.3 %collective-permute-start.9 = (bf16[32,3712]{1,0:T(8,128)(2,1)S(1)}, bf16[32,3712]{1,0:T(8,128)(2,1)S(1)}, u32[]{:S(2)}, u32[]{:S(2)}) collective-permute-start(bf16[32,3712]{1,0:T(8,128)(2,1)S(1)} %collective-permute-done.8.refs_6_), channel_id=1, source_target_pairs={{0,16},{16,128},{128,144},{144,0},{1,145},{17,1},{129,17},{145,129... | collective-permute-start | bytes 712712 | tf_op jit(solution)/shard_map/ppermute | solution.py:236
  50.0 6.8 %collective-permute-start.11 = (bf16[32,3712]{1,0:T(8,128)(2,1)S(1)}, bf16[32,3712]{1,0:T(8,128)(2,1)S(1)}, u32[]{:S(2)}, u32[]{:S(2)}) collective-permute-start(bf16[32,3712]{1,0:T(8,128)(2,1)S(1)} %collective-permute-done.10.refs_8_), channel_id=1, source_target_pairs={{0,16},{16,128},{128,144},{144,0},{1,145},{17,1},{129,17},{145,129... | collective-permute-start | bytes 712712 | tf_op jit(solution)/shard_map/ppermute | solution.py:236
  50.7 10.0 %collective-permute-start.15 = (bf16[32,3712]{1,0:T(8,128)(2,1)S(1)}, bf16[32,3712]{1,0:T(8,128)(2,1)S(1)}, u32[]{:S(2)}, u32[]{:S(2)}) collective-permute-start(bf16[32,3712]{1,0:T(8,128)(2,1)S(1)} %broadcast_select_fusion.1.refs_12_), channel_id=1, source_target_pairs={{0,16},{16,128},{128,144},{144,0},{1,145},{17,1},{129,17},{145,129... | collective-permute-start | bytes 712712 | tf_op jit(solution)/shard_map/ppermute | solution.py:236
  50.9 9.7 %collective-permute-start.13 = (bf16[32,3712]{1,0:T(8,128)(2,1)S(1)}, bf16[32,3712]{1,0:T(8,128)(2,1)}, u32[]{:S(2)}, u32[]{:S(2)}) collective-permute-start(bf16[32,3712]{1,0:T(8,128)(2,1)S(1)} %collective-permute-done.12.refs_10_), channel_id=1, source_target_pairs={{0,16},{16,128},{128,144},{144,0},{1,145},{17,1},{129,17},{145,129... | collective-permute-start | bytes 712712 | tf_op jit(solution)/shard_map/ppermute | solution.py:236
  53.0 10.2 %collective-permute-start.17 = (bf16[32,3712]{1,0:T(8,128)(2,1)S(1)}, bf16[32,3712]{1,0:T(8,128)(2,1)}, u32[]{:S(2)}, u32[]{:S(2)}) collective-permute-start(bf16[32,3712]{1,0:T(8,128)(2,1)S(1)} %broadcast_select_fusion.refs_14_), channel_id=1, source_target_pairs={{0,16},{16,128},{128,144},{144,0},{1,145},{17,1},{129,17},{145,129... | collective-permute-start | bytes 712712 | tf_op jit(solution)/shard_map/ppermute | solution.py:236
